TPU v7x, 32 devices: a whole 2x2x4 slice. The times are simulated.
32 devices in a mesh: det: 4 (over y, core), tm: 8 (over z, x).
Axes of the slice: x: 2, y: 2, z: 4, core: 2. Of those that a mesh axis runs over, the one named last changes fastest.
Arguments:
- spectra: bfloat16 [4, 16, 32, 2, 128], P('det', 'tm'), may hold values from -200 to 200
- valid: int32 [16], P('tm'), may hold values 0 or 1
- lags: float32 [49152], replicated, may hold values from -0.01 to 0.01
- drift: float32 [49152], replicated, may hold values from -4 to 4
- block_table: int32 [64, 2], replicated, may hold values from 0 to 95, as said below
Outputs:
- sky_map: float32 [49152], P(('det', 'tm'))
Inputs may be any that keep to these rules, and one draw needn't show every extreme that they name: `block_table`: row (2 i + h) * 4 + k, for 0 <= i < 8, h in 0, 1 and 0 <= k < 4, holds a band from h * 32 to h * 32 + 31 and a tile below 96; each aligned block of 2 rows starting at a multiple of 2 has one band, and the 2 bands of one (i, h) are distinct.
All inputs are finite; a program needn't handle non-finite values. No bound on the sum of `valid` on one device may be relied on, other than what follows from the above.
Results may differ from a plain program's by a relative error of at most 0.0037.
Values may be sent and summed in bfloat16 or wider, within the bound.
No kernel may reach another device: no remote copies, remote signals or barrier semaphores. Data moves between devices by JAX's collectives and lax.ppermute only.
A program may use at most 64 MiB of HBM per device.

v0:
```python
import math

import jax
import jax.numpy as jnp
from jax import lax
from jax.sharding import PartitionSpec as P

PT = 512
TPB = 2


full_turn = 2.0 * math.pi


def from_partner(x, axis, distance):
    return lax.ppermute(x, axis, [(i, i ^ 1 << distance) for i in range(lax.axis_size(axis))])


def tile_partial(band_slab, band_id, pixel_lags, pixel_drift, time_coord, band_total, band_width):
    frequency = (band_id * band_width + jnp.arange(band_width, dtype=jnp.int32)).astype(jnp.float32)
    angle_grid = full_turn * frequency[:, None] * pixel_lags[None, :]
    cosine_grid = jnp.cos(angle_grid)
    sine_grid = jnp.sin(angle_grid)
    kernel = jnp.concatenate(
        [
            jnp.concatenate([cosine_grid, -sine_grid], 1),
            jnp.concatenate([sine_grid, cosine_grid], 1),
        ],
        0,
    ).astype(jnp.bfloat16)
    product = jnp.dot(band_slab, kernel, preferred_element_type=jnp.float32)
    columns = pixel_lags.shape[0]
    factor = full_turn * (band_id.astype(jnp.float32) + 0.5) / band_total
    rotation = (factor * pixel_drift)[None, :] * time_coord[:, None]
    return jnp.sum(
        jnp.cos(rotation) * product[:, :columns] - jnp.sin(rotation) * product[:, columns:], axis=0
    )


def shards(spectra, valid, lags, drift, block_table):
    det_index = lax.axis_index("det")
    bin_half = det_index % 2
    detector_bit = det_index // 2
    tm_count = lax.axis_size("tm")
    tm_index = lax.axis_index("tm")
    own_spectra = spectra[0]
    seg_count = own_spectra.shape[0]
    bands_half = own_spectra.shape[1]
    band_width = own_spectra.shape[3]
    seg_kept = seg_count // 2
    segment_total = seg_count * tm_count
    band_total = 2 * bands_half
    squares = jnp.sum(jnp.square(own_spectra.astype(jnp.float32)), axis=(1, 2, 3))
    stacked = jnp.stack(
        [jnp.where(detector_bit == 0, squares, 0.0), jnp.where(detector_bit == 1, squares, 0.0)]
    )
    powers = lax.psum(stacked, "det") / (band_total * band_width) + 1e-06
    seg_start = detector_bit * seg_kept
    kept_rows = lax.dynamic_slice_in_dim(own_spectra, seg_start, seg_kept, 0)
    sent_rows = lax.dynamic_slice_in_dim(own_spectra, seg_kept - seg_start, seg_kept, 0)
    arrived = from_partner(sent_rows, "det", 1)
    hanford = jnp.where(detector_bit == 0, kept_rows, arrived).astype(jnp.float32)
    livingston = jnp.where(detector_bit == 0, arrived, kept_rows).astype(jnp.float32)
    kept_powers = lax.dynamic_slice_in_dim(powers, seg_start, seg_kept, 1)
    valid_rows = lax.dynamic_slice_in_dim(valid, seg_start, seg_kept, 0).astype(jnp.float32)
    weight = valid_rows / (kept_powers[0] * kept_powers[1])
    cross_real = (
        hanford[:, :, 0] * livingston[:, :, 0] + hanford[:, :, 1] * livingston[:, :, 1]
    ) * weight[:, None, None]
    cross_imag = (
        hanford[:, :, 0] * livingston[:, :, 1] - hanford[:, :, 1] * livingston[:, :, 0]
    ) * weight[:, None, None]
    cross = (
        jnp.stack([cross_real, cross_imag], 2)
        .astype(jnp.bfloat16)
        .reshape(seg_kept, bands_half, 2 * band_width)
    )
    by_band = jnp.transpose(cross, (1, 0, 2))
    blocks_all = block_table.reshape(tm_count, 2, -1, 2)
    chosen = lax.dynamic_index_in_dim(blocks_all, bin_half, 1, keepdims=False)
    own_blocks = lax.dynamic_index_in_dim(chosen, tm_index, 0, keepdims=False)
    block_count = own_blocks.shape[0]
    picked = chosen[:, ::TPB, 0] - bin_half * bands_half
    outgoing = jnp.take(by_band, picked.reshape(-1), axis=0).reshape(
        tm_count, picked.shape[1], seg_kept, 2 * band_width
    )
    received = lax.all_to_all(outgoing, "tm", split_axis=0, concat_axis=2, tiled=True)
    item_bands = own_blocks[::TPB, 0]
    item_tiles = own_blocks[:, 1].reshape(-1, TPB)
    row_ids = jnp.arange(tm_count * seg_kept, dtype=jnp.int32)
    segment_ids = row_ids // seg_kept * seg_count + detector_bit * seg_kept + row_ids % seg_kept
    time_coord = (segment_ids.astype(jnp.float32) + 0.5 - segment_total / 2) / segment_total

    def one_item(item):
        band_slab, band_id, tile_ids = item
        pixels = (tile_ids[:, None] * PT + jnp.arange(PT, dtype=jnp.int32)[None, :]).reshape(-1)
        return tile_partial(
            band_slab,
            band_id,
            jnp.take(lags, pixels),
            jnp.take(drift, pixels),
            time_coord,
            band_total,
            band_width,
        )

    partials = lax.map(one_item, (received[0], item_bands, item_tiles)).reshape(block_count, -1)
    tile_total = lags.shape[0] // PT
    onehot = (own_blocks[:, 1][:, None] == jnp.arange(tile_total, dtype=jnp.int32)[None, :]).astype(
        jnp.float32
    )
    sky_map = jnp.dot(
        onehot.T, partials, precision=lax.Precision.HIGHEST, preferred_element_type=jnp.float32
    ).reshape(-1)
    summed = lax.psum(sky_map, ("det", "tm"))
    per_device = summed.shape[0] // (lax.axis_size("det") * tm_count)
    result = lax.dynamic_slice_in_dim(
        summed, (det_index * tm_count + tm_index) * per_device, per_device
    )
    return result / math.sqrt(segment_total * band_width)


def solution(mesh):
    placed = (P("det", "tm", None, None, None), P("tm"), P(), P(), P())
    return jax.shard_map(
        shards, mesh=mesh, in_specs=placed, out_specs=P(("det", "tm")), check_vma=False
    )
```

profile of v0, /device:TPU:0, one launch (start us, length us, event | category | flops | bytes accessed | tf_op | source)
XLA Modules:
  0.0 201.2 jit_solution(12568904724620629175)
XLA Ops:
  6.5 0.8 dynamic-slice_bitcast_fusion
  7.3 3.1 %collective-permute-start = (bf16[1,32,2,128]{3,2,1,0:T(2,128)(2,1)S(1)}, bf16[1,32,2,128]{3,2,1,0:T(2,128)(2,1)S(1)}, u32[]{:S(2)}, u32[]{:S(2)}) collective-permute-start(bf16[1,32,2,128]{3,2,1,0:T(2,128)(2,1)S(1)} %dynamic-slice_bitcast_fusion), channel_id=1, source_target_pairs={{0,16},{8,24},{16,0},{24,8},{1,17},{9,25},{17,1},{25,9},{2,18},{10... | collective-permute-start | bytes 49160 | tf_op jit(solution)/shard_map/ppermute | solution.py:16
  10.4 0.9 multiply_reduce_fusion
  11.3 5.8 %psum.14 = f32[2,2]{1,0:T(2,128)S(1)} all-reduce(f32[2,2]{1,0:T(2,128)S(1)} %pad_maximum_fusion.1), channel_id=1, replica_groups=mesh['det'=4,'tm'=8] {'det'}, use_global_device_ids=true, to_apply=%region_1.2 | all-reduce | flops 4 | bytes 32 | tf_op jit(solution)/shard_map/psum | solution.py:57
  17.2 0.5 fusion.29
  17.7 0.8 reshape.179
  18.9 1.2 dynamic_slice.54
  22.3 0.6 gather_fusion.2
  22.9 0.7 broadcast_select_fusion.3
  23.6 5.9 %all-to-all-start = ((bf16[8,2,1,256]{3,1,2,0:T(2,128)(2,1)}), bf16[8,2,1,256]{3,1,2,0:T(2,128)(2,1)S(1)}, u32[]{:S(2)}, u32[]{:S(2)}) async-start(bf16[8,2,1,256]{3,1,2,0:T(2,128)(2,1)} %broadcast_select_fusion.3), calls=%async_computation | async-start | bytes 16384 | tf_op jit(solution)/shard_map/all_to_all | solution.py:87
  29.7 6.3 %all-to-all-done = bf16[8,2,1,256]{3,1,2,0:T(2,128)(2,1)S(1)} async-done(((bf16[8,2,1,256]{3,1,2,0:T(2,128)(2,1)}), bf16[8,2,1,256]{3,1,2,0:T(2,128)(2,1)S(1)}, u32[]{:S(2)}, u32[]{:S(2)}) %all-to-all-start) | async-done | bytes 8224 | tf_op jit(solution)/shard_map/all_to_all | solution.py:87
  36.0 34.3 %while.13 = (s32[]{:T(128)}, f32[2,1024]{1,0:T(2,128)S(1)}, s32[2]{0:T(128)S(1)}, s32[2,2]{1,0:T(2,128)S(1)}, f32[49152]{0:T(1024)S(1)}, /*index=5*/bf16[2,8,256...) while((s32[]{:T(128)}, f32[2,1024]{1,0:T(2,128)S(1)}, ...), condition=%wide.region_4.6_spmd.clone, body=%wide.region_2.5_spmd.clone.sunk | while | flops 13292976 | bytes 1797413 | solution.py:107
  36.1 6.1 %gather_fusion = f32[1024]{0:T(1024)S(1)} fusion(f32[49152]{0:T(1024)S(1)} %get-tuple-element.257, s32[1024]{0:T(1024)S(1)} %fusion.39), kind=kCustom, calls=%fused_computation.clone.clone.1 | custom fusion | bytes 12288 | tf_op jit(solution)/shard_map/while/body/eval_jaxpr/jit(_take)/gather | solution.py:101
  42.3 0.6 dynamic_slice.77
  43.5 6.2 %gather_fusion.1 = f32[1024]{0:T(1024)S(1)} fusion(f32[49152]{0:T(1024)S(1)} %get-tuple-element.259, s32[1024]{0:T(1024)S(1)} %fusion.39), kind=kCustom, calls=%fused_computation.1.clone.clone.1 | custom fusion | bytes 12288 | tf_op jit(solution)/shard_map/while/body/eval_jaxpr/jit(_take)/gather | solution.py:100
  50.4 2.2 %fusion.40 = (bf16[128,1024]{1,0:T(8,128)(2,1)S(1)}, bf16[128,1024]{1,0:T(8,128)(2,1)S(1)}, bf16[128,1024]{1,0:T(8,128)(2,1)S(1)}) fusion(f32[1024]{0:T(1024)S(1)} %broadcast_select_fusion.7, f32[128]{0:T(128)S(1)} %convert_multiply_fusion.2), kind=kLoop, calls=%fused_computation.16.clone.1 | loop fusion | flops 655360 | bytes 791040 | tf_op jit(solution)/shard_map/convert.5
  53.3 6.1 %gather_fusion = f32[1024]{0:T(1024)S(1)} fusion(f32[49152]{0:T(1024)S(1)} %get-tuple-element.257, s32[1024]{0:T(1024)S(1)} %fusion.39), kind=kCustom, calls=%fused_computation.clone.clone.1 | custom fusion | bytes 12288 | tf_op jit(solution)/shard_map/while/body/eval_jaxpr/jit(_take)/gather | solution.py:101
  59.4 0.6 dynamic_slice.77
  60.7 6.2 %gather_fusion.1 = f32[1024]{0:T(1024)S(1)} fusion(f32[49152]{0:T(1024)S(1)} %get-tuple-element.259, s32[1024]{0:T(1024)S(1)} %fusion.39), kind=kCustom, calls=%fused_computation.1.clone.clone.1 | custom fusion | bytes 12288 | tf_op jit(solution)/shard_map/while/body/eval_jaxpr/jit(_take)/gather | solution.py:100
  67.5 2.2 %fusion.40 = (bf16[128,1024]{1,0:T(8,128)(2,1)S(1)}, bf16[128,1024]{1,0:T(8,128)(2,1)S(1)}, bf16[128,1024]{1,0:T(8,128)(2,1)S(1)}) fusion(f32[1024]{0:T(1024)S(1)} %broadcast_select_fusion.7, f32[128]{0:T(128)S(1)} %convert_multiply_fusion.2), kind=kLoop, calls=%fused_computation.16.clone.1 | loop fusion | flops 655360 | bytes 791040 | tf_op jit(solution)/shard_map/convert.5
  70.3 0.4 convolution_bitcast_fusion
  70.7 0.7 copy.19
  71.4 121.6 %all-reduce.2.cloned.1.call-done = f32[49152]{0:T(1024)} async-done(((f32[49152]{0:T(1024)}), f32[49152]{0:T(1024)}) %all-reduce.2.cloned.1.call-update) | async-done | bytes 196624 | tf_op jit(solution)/shard_map/psum | solution.py:115
  193.0 1.4 dynamic-slice_multiply_fusion
  (56 shorter events, 2.2 us)
Async XLA Ops:
  6.5 15.5 %copy-start.2 = (bf16[1,2,32,2,128]{4,3,2,1,0:T(2,128)(2,1)S(1)}, bf16[1,2,32,2,128]{4,3,2,1,0:T(2,128)(2,1)}, u32[]{:S(2)}) copy-start(bf16[1,2,32,2,128]{4,3,2,1,0:T(2,128)(2,1)} %param.9) | copy-start | bytes 98308
  7.3 14.7 %collective-permute-start = (bf16[1,32,2,128]{3,2,1,0:T(2,128)(2,1)S(1)}, bf16[1,32,2,128]{3,2,1,0:T(2,128)(2,1)S(1)}, u32[]{:S(2)}, u32[]{:S(2)}) collective-permute-start(bf16[1,32,2,128]{3,2,1,0:T(2,128)(2,1)S(1)} %dynamic-slice_bitcast_fusion), channel_id=1, source_target_pairs={{0,16},{8,24},{16,0},{24,8},{1,17},{9,25},{17,1},{25,9},{2,18},{10... | collective-permute-start | bytes 49160 | tf_op jit(solution)/shard_map/ppermute | solution.py:16
  18.5 17.5 %copy-start = (f32[49152]{0:T(1024)S(1)}, f32[49152]{0:T(1024)}, u32[]{:S(2)}) copy-start(f32[49152]{0:T(1024)} %param.12) | copy-start | bytes 589828
  18.5 17.5 %copy-start.1 = (f32[49152]{0:T(1024)S(1)}, f32[49152]{0:T(1024)}, u32[]{:S(2)}) copy-start(f32[49152]{0:T(1024)} %param.11) | copy-start | bytes 589828
  23.6 12.4 %all-to-all-start = ((bf16[8,2,1,256]{3,1,2,0:T(2,128)(2,1)}), bf16[8,2,1,256]{3,1,2,0:T(2,128)(2,1)S(1)}, u32[]{:S(2)}, u32[]{:S(2)}) async-start(bf16[8,2,1,256]{3,1,2,0:T(2,128)(2,1)} %broadcast_select_fusion.3), calls=%async_computation | async-start | bytes 16384 | tf_op jit(solution)/shard_map/all_to_all | solution.py:87
  29.5 163.5 %all-reduce.2.cloned.1.call-start = ((), (), s32[]{:S(2)}) async-start(), calls=%async_computation.1 | async-start | bytes 393216 | tf_op jit(solution)/shard_map/psum | solution.py:115
Sparse Core Ops, SparseCore 0:
  71.5 121.3 all-reduce.1
where the time goes:
time: 202 us; the launch traced here: 201 us
  waiting for transfers between devices  128 us (63%)
  local copies, waits for them, and re-layouts  31.3 us (15%)
  between operations  15.4 us (8%)
  starting transfers between devices  9.02 us (4%)
  other arithmetic  8.26 us (4%)
  blocking collectives  5.76 us (3%)
  loops' own time  2.76 us (1%)
    psum x1, waiting for transfers between devices, shards(): summed = lax.psum(sky_map, ('det', 'tm'))  122 us
    gather x2, local copies, waits for them, and re-layouts, one_item(): jnp.take(lags, pixels)  12.3 us
    gather x2, local copies, waits for them, and re-layouts, one_item(): jnp.take(drift, pixels)  12.3 us
    all_to_all x1, waiting for transfers between devices, shards(): lax.all_to_all(outgoing, 'tm', split_axis=0, concat_axis=2, tiled=True)  6.28 us
    all_to_all x1, starting transfers between devices, shards(): lax.all_to_all(outgoing, 'tm', split_axis=0, concat_axis=2, tiled=True)  5.93 us
    psum x1, blocking collectives, shards(): powers = lax.psum(stacked, 'det') / (band_total * band_width) + 1e-06  5.76 us
    another operation x3, other arithmetic  4.51 us
  transfers between devices with their start and end apart: 3, of which 2 were waited for; matrix products, arithmetic and copies ran while one was open for 2% of the time, Pallas kernels for 0%

commit v1 on v0

v1 whole, which is shorter than its diff:
```python
import functools
import math

import jax
import jax.numpy as jnp
import numpy as np
from jax import lax
from jax.experimental import pallas as pl
from jax.experimental.pallas import tpu as pltpu
from jax.sharding import PartitionSpec as P

PT = 512
TPB = 2
LANES = 128
INNER = 16
PARTS = 6

NEAR_COS = (0.9999999994443334, -19.739207715972064, 64.93905415215964, -85.41956519425082, 58.57456432893444)
NEAR_SIN = (6.283185306861161, -41.341701618023556, 81.60505457483515, -76.68452620857785, 41.10289536853278)
VMEM = pl.BlockSpec(memory_space=pltpu.VMEM)
SMEM = pl.BlockSpec(memory_space=pltpu.SMEM)


def fitted(function, limit, degree):
    nodes = (np.cos(np.pi * (np.arange(400) + 0.5) / 400) + 1) / 2
    powers = np.vander(nodes, degree + 1, increasing=True)
    coefficients = np.linalg.lstsq(powers, function(np.sqrt(nodes * limit)), rcond=None)[0]
    return tuple(float(c) for c in coefficients / limit ** np.arange(degree + 1))


FAR_COS = fitted(lambda r: np.cos(2 * np.pi * r), 0.25, 6)
FAR_SIN = fitted(lambda r: np.sin(2 * np.pi * r) / r, 0.25, 6)


def horner(coefficients, z):
    total = jnp.full_like(z, coefficients[-1])
    for c in coefficients[-2::-1]:
        total = total * z + c
    return total


def near_turn(x):
    z = x * x
    return horner(NEAR_COS, z), x * horner(NEAR_SIN, z)


def any_turn(x):
    r = x - jnp.floor(x + 0.5)
    z = r * r
    return horner(FAR_COS, z), r * horner(FAR_SIN, z)


def split(x):
    high = x.astype(jnp.bfloat16)
    return high, (x - high.astype(jnp.float32)).astype(jnp.bfloat16)


def terms_kernel(
    tm_count, rows_dest, seg_kept,
    place_ref, valid_ref, table_ref, own_ref, other_ref, lags_ref, drift_ref,
    out_ref,
    own32, other32, cross, masked, left, total,
):
    det_index, tm_index = place_ref[0], place_ref[1]
    bin_half = det_index % 2
    detector_bit = det_index // 2
    bands_half = own_ref.shape[1] // 2
    width = own_ref.shape[2]
    outer = width // INNER
    seg_count = own_ref.shape[0]
    segment_total = seg_count * tm_count
    band_total = 2 * bands_half
    per_group = table_ref.shape[1] // (2 * tm_count)
    slots = tm_count * per_group // TPB
    per_tile = PT // LANES
    flip = jnp.where(detector_bit == 0, 1.0, -1.0).astype(jnp.float32)
    outer_at = lax.broadcasted_iota(jnp.int32, (outer, width), 0)
    lane_at = lax.broadcasted_iota(jnp.int32, (outer, width), 1)
    mask = (lane_at // INNER == outer_at).astype(jnp.float32)
    from_lane = lax.broadcasted_iota(jnp.int32, (width, LANES), 0) % INNER
    to_lane = lax.broadcasted_iota(jnp.int32, (width, LANES), 1)
    same = from_lane == to_lane % INNER
    part = to_lane // INNER

    def chooser(*parts):
        chosen = part == parts[0]
        for p in parts[1:]:
            chosen = chosen | (part == p)
        return (same & chosen).astype(jnp.float32).astype(jnp.bfloat16)

    choose = jnp.concatenate([chooser(0, 4), chooser(1, 5), chooser(2), chooser(3)], 0)
    inner_at = lax.broadcasted_iota(jnp.int32, (INNER, PT), 0).astype(jnp.float32)
    start_at = (lax.broadcasted_iota(jnp.int32, (outer, PT), 0) * INNER).astype(jnp.float32)
    total[...] = jnp.zeros_like(total)

    for s in range(seg_kept):
        seg = detector_bit * seg_kept + s
        own32[...] = own_ref[seg].astype(jnp.float32)
        other32[...] = other_ref[seg].astype(jnp.float32)
        own_r = own32[pl.ds(0, bands_half, stride=2), :]
        own_i = own32[pl.ds(1, bands_half, stride=2), :]
        other_r = other32[pl.ds(0, bands_half, stride=2), :]
        other_i = other32[pl.ds(1, bands_half, stride=2), :]
        cross[0] = own_r * other_r + own_i * other_i
        cross[1] = (own_r * other_i - own_i * other_r) * flip
        for b in range(bands_half):
            real = jnp.broadcast_to(cross[0, b : b + 1, :], (outer, width)) * mask
            imag = jnp.broadcast_to(cross[1, b : b + 1, :], (outer, width)) * mask
            high, low = split(jnp.concatenate([real, imag], 0))
            high_t, low_t = split(jnp.concatenate([imag, -real], 0))
            masked[b] = jnp.concatenate([high, high_t, low, low_t], 1)
        stacked = masked[...].reshape(bands_half * 2 * outer, 4 * width)
        left[...] = (
            jnp.dot(stacked, choose, preferred_element_type=jnp.float32)
            .astype(jnp.bfloat16)
            .reshape(bands_half, 2 * outer, LANES)
        )
        time_coord = ((tm_index * seg_count + seg).astype(jnp.float32) + 0.5 - segment_total / 2) / segment_total
        live = valid_ref[seg].astype(jnp.float32)

        def one_slot(slot, _):
            group = slot * TPB // per_group
            row = (2 * group + bin_half) * per_group + slot * TPB % per_group
            band = table_ref[0, row]
            lhs = left[band - bin_half * bands_half][:, : PARTS * INNER]
            turn = (band.astype(jnp.float32) + 0.5) / band_total * time_coord
            frequency = (band * width).astype(jnp.float32) + start_at
            for m in range(TPB):
                tile = table_ref[1, row + m]
                lag = jnp.concatenate([lags_ref[tile, c : c + 1, :] for c in range(per_tile)], 1)
                pace = jnp.concatenate([drift_ref[tile, c : c + 1, :] for c in range(per_tile)], 1)
                cosine, sine = near_turn(jnp.broadcast_to(lag, (INNER, PT)) * inner_at)
                cos_high, cos_low = split(cosine)
                sin_high, sin_low = split(sine)
                rhs = jnp.concatenate([cos_high, sin_high, cos_high, sin_high, cos_low, sin_low], 0)
                product = jnp.dot(lhs, rhs, preferred_element_type=jnp.float32)
                angle = jnp.broadcast_to(pace * turn, (outer, PT)) - frequency * jnp.broadcast_to(lag, (outer, PT))
                cosine, sine = any_turn(angle)
                terms = jnp.sum(cosine * product[:outer] - sine * product[outer:], axis=0, keepdims=True) * live
                for c in range(per_tile):
                    at = tile * per_tile + c
                    where = at // rows_dest, s, pl.ds(at % rows_dest, 1)
                    total[where] += terms[:, c * LANES : (c + 1) * LANES]
            return 0

        lax.fori_loop(0, slots, one_slot, 0)
        for n, data in enumerate((own32, other32)):
            power = jnp.sum(jnp.sum(data[...] * data[...], axis=0, keepdims=True), axis=1, keepdims=True)
            high = power.astype(jnp.bfloat16).astype(jnp.float32)
            for p, value in enumerate((high, power - high)):
                where = slice(None), s, pl.ds(rows_dest + 2 * n + p, 1)
                total[where] = jnp.broadcast_to(value.reshape(1, 1, 1), (total.shape[0], 1, LANES))
    out_ref[...] = total[...].astype(jnp.bfloat16)


def weights_of(power, fourier_bins):
    halves = power[..., 0::2, :] + power[..., 1::2, :]
    whole = halves.reshape(2, 2, *halves.shape[1:]).sum(1) / fourier_bins + 1e-06
    return 1.0 / (whole[..., 0, :] * whole[..., 1, :])


def sum_kernel(tm_count, rows_dest, fourier_bins, scale, got_ref, out_ref):
    seg_kept = got_ref.shape[1]
    total = jnp.zeros((rows_dest, LANES), jnp.float32)
    for k in range(2):
        for i in range(tm_count):
            for s in range(seg_kept):
                pair = [got_ref[(2 * k + h) * tm_count + i, s].astype(jnp.float32) for h in range(2)]
                both = pair[0] + pair[1]
                own = (both[rows_dest : rows_dest + 1] + both[rows_dest + 1 : rows_dest + 2]) / fourier_bins + 1e-06
                other = (both[rows_dest + 2 : rows_dest + 3] + both[rows_dest + 3 : rows_dest + 4]) / fourier_bins + 1e-06
                total = total + both[:rows_dest] * (1.0 / (own * other))
    out_ref[...] = total / scale


def shards(spectra, valid, lags, drift, block_table):
    det_count, tm_count = lax.axis_size("det"), lax.axis_size("tm")
    devices = det_count * tm_count
    own = spectra[0]
    seg_count, bands_half, _, width = own.shape
    seg_kept = seg_count // 2
    pixels = lags.shape[0]
    per_device = pixels // devices
    fourier_bins = 2 * bands_half * width
    scale = math.sqrt(seg_count * tm_count * width)
    direct = per_device % LANES == 0
    rows_dest = (per_device if direct else pixels) // LANES
    dests = devices if direct else 1
    rows = -(-(rows_dest + 4) // 8) * 8
    per_tile = PT // LANES

    own = own.reshape(seg_count, 2 * bands_half, width)
    other = lax.ppermute(own, "det", [(d, d ^ 2) for d in range(det_count)])
    place = jnp.stack([lax.axis_index("det"), lax.axis_index("tm")]).astype(jnp.int32)
    outgoing = pl.pallas_call(
        functools.partial(terms_kernel, tm_count, rows_dest, seg_kept),
        out_shape=jax.ShapeDtypeStruct((dests, seg_kept, rows, LANES), jnp.bfloat16),
        in_specs=[SMEM] * 3 + [VMEM] * 4,
        out_specs=VMEM,
        scratch_shapes=[
            pltpu.VMEM((2 * bands_half, width), jnp.float32),
            pltpu.VMEM((2 * bands_half, width), jnp.float32),
            pltpu.VMEM((2, bands_half, width), jnp.float32),
            pltpu.VMEM((bands_half, 2 * width // INNER, 4 * width), jnp.bfloat16),
            pltpu.VMEM((bands_half, 2 * width // INNER, LANES), jnp.bfloat16),
            pltpu.VMEM((dests, seg_kept, rows, LANES), jnp.float32),
        ],
        name="terms",
    )(place, valid, block_table.T, own, other, lags.reshape(-1, per_tile, LANES), drift.reshape(-1, per_tile, LANES))
    if direct:
        received = lax.all_to_all(outgoing, ("det", "tm"), 0, 0, tiled=True)
        result = pl.pallas_call(
            functools.partial(sum_kernel, tm_count, rows_dest, fourier_bins, scale),
            out_shape=jax.ShapeDtypeStruct((rows_dest, LANES), jnp.float32),
            in_specs=[VMEM],
            out_specs=VMEM,
            name="sum",
        )(received)
        return result.reshape(-1)
    maps = jnp.moveaxis(outgoing[0, :, :rows_dest].reshape(seg_kept, devices, per_device), 1, 0)
    powers = jnp.broadcast_to(outgoing[0, :, rows_dest : rows_dest + 4, 0], (devices, seg_kept, 4))
    sent = jnp.concatenate([maps, powers], 2)
    received = lax.all_to_all(sent, ("det", "tm"), 0, 0, tiled=True).astype(jnp.float32)
    received = received.reshape(det_count, tm_count, seg_kept, per_device + 4)
    weight = weights_of(received[..., per_device:, None], fourier_bins)[..., 0]
    both = received[..., :per_device].reshape(2, 2, tm_count, seg_kept, per_device).sum(1)
    return (both * weight[..., None]).sum((0, 1, 2)) / scale


def solution(mesh):
    placed = (P("det", "tm", None, None, None), P("tm"), P(), P(), P())
    return jax.shard_map(
        shards, mesh=mesh, in_specs=placed, out_specs=P(("det", "tm")), check_vma=False
    )
```

time: 202 us -> 27.2 us (0.13)
  waiting for transfers between devices: 128 us -> 1.45 us
  local copies, waits for them, and re-layouts: 31.3 us -> 0.61 us
  between operations: 15.4 us -> 0.01 us
  blocking collectives: 5.76 us -> 14.3 us
  other arithmetic: 8.26 us -> 0.65 us
  Pallas kernels: 0 us -> 7.04 us
  starting transfers between devices: 9.02 us -> 3 us
  loops' own time: 2.76 us -> 0 us
    psum x1 -> x0, waiting for transfers between devices: 122 us -> none  [shards(): summed = lax.psum(sky_map, ('det', 'tm'))]
    gather x6 -> x0, local copies, waits for them, and re-layouts: 25.2 us -> none  [the longest x2 12.3 us: one_item(): jnp.take(lags, pixels)]
    all_to_all x0 -> x1, blocking collectives: none -> 14.3 us  [shards(): received = lax.all_to_all(outgoing, ('det', 'tm'), 0, 0, tiled=True)]
    pallas_call x0 -> x2, Pallas kernels: none -> 7.04 us  [the longest x1 5.5 us: shards(): pl.pallas_call(functools.partial(terms_kernel, tm_count, rows_dest, seg_k...]
    all_to_all x1 -> x0, waiting for transfers between devices: 6.28 us -> none  [shards(): lax.all_to_all(outgoing, 'tm', split_axis=0, concat_axis=2, tiled=True)]
    all_to_all x1 -> x0, starting transfers between devices: 5.93 us -> none  [shards(): lax.all_to_all(outgoing, 'tm', split_axis=0, concat_axis=2, tiled=True)]
    psum x1 -> x0, blocking collectives: 5.76 us -> none  [shards(): powers = lax.psum(stacked, 'det') / (band_total * band_width) + 1e-06]
    another operation x5 -> x1, other arithmetic: 4.56 us -> 0.65 us  [shards(): jnp.stack([lax.axis_index('det'), lax.axis_index('tm')]).astype(jnp.int32)]
  transfers between devices with their start and end apart: 3 -> 1, of which waited for: 2 -> 1; matrix products, arithmetic and copies ran while one was open for 2% -> 2% of each run, Pallas kernels for 0% -> 0%
where the time goes in v1:
time: 27.2 us; the launch traced here: 27 us
  blocking collectives  14.3 us (53%)
  Pallas kernels  7.04 us (26%)
  starting transfers between devices  3 us (11%)
  waiting for transfers between devices  1.45 us (5%)
  other arithmetic  0.65 us (2%)
  local copies, waits for them, and re-layouts  0.61 us (2%)
    all_to_all x1, blocking collectives, shards(): received = lax.all_to_all(outgoing, ('det', 'tm'), 0, 0, tiled=True)  14.3 us
    pallas_call x1, Pallas kernels, shards(): pl.pallas_call(functools.partial(terms_kernel, tm_count, rows_dest, seg_k...  5.5 us
    ppermute x1, starting transfers between devices, shards(): other = lax.ppermute(own, 'det', [(d, d ^ 2) for d in range(det_count)])  3 us
    pallas_call x1, Pallas kernels, shards(): pl.pallas_call(functools.partial(sum_kernel, tm_count, rows_dest, fourier...  1.55 us
    ppermute x1, waiting for transfers between devices, shards(): other = lax.ppermute(own, 'det', [(d, d ^ 2) for d in range(det_count)])  1.45 us
    another operation x1, other arithmetic, shards(): jnp.stack([lax.axis_index('det'), lax.axis_index('tm')]).astype(jnp.int32)  0.65 us
    unnamed x2, local copies, waits for them, and re-layouts  0.61 us
  transfers between devices with their start and end apart: 1, of which 1 were waited for; matrix products, arithmetic and copies ran while one was open for 2% of the time, Pallas kernels for 0%

profile of v1, /device:TPU:0, one launch (start us, length us, event | category | flops | bytes accessed | tf_op | source)
XLA Modules:
  0.0 27.0 jit_solution(660254308404156017)
XLA Ops:
  0.0 3.0 %collective-permute-start = (bf16[2,64,128]{2,1,0:T(8,128)(2,1)}, bf16[2,64,128]{2,1,0:T(8,128)(2,1)S(1)}, u32[]{:S(2)}, u32[]{:S(2)}) collective-permute-start(bf16[2,64,128]{2,1,0:T(8,128)(2,1)} %bitcast.9), channel_id=1, source_target_pairs={{0,16},{8,24},{16,0},{24,8},{1,17},{9,25},{17,1},{25,9},{2,18},{10... | collective-permute-start | bytes 98312 | tf_op jit(solution)/shard_map/ppermute | solution.py:193
  3.0 0.6 %pad_add_fusion.place_ref = s32[2]{0:T(128)} fusion(s32[1]{0:T(128)} %bitcast.1, s32[1]{0:T(128)} %bitcast), kind=kLoop, calls=%fused_computation | loop fusion | flops 2 | bytes 16 | tf_op jit(solution)/shard_map/stack | solution.py:194
  3.6 1.5 %collective-permute-done.other_ref = bf16[2,64,128]{2,1,0:T(8,128)(2,1)S(1)} collective-permute-done((bf16[2,64,128]{2,1,0:T(8,128)(2,1)}, bf16[2,64,128]{2,1,0:T(8,128)(2,1)S(1)}, u32[]{:S(2)}, u32[]{:S(2)}) %collective-permute-start) | collective-permute-done | bytes 32800 | tf_op jit(solution)/shard_map/ppermute | solution.py:193
  5.1 0.0 copy-start
  5.1 0.6 %copy-done = bf16[2,64,128]{2,1,0:T(8,128)(2,1)} copy-done((bf16[2,64,128]{2,1,0:T(8,128)(2,1)}, bf16[2,64,128]{2,1,0:T(8,128)(2,1)S(1)}, u32[]{:S(2)}) %copy-start) | copy-done | bytes 32792
  5.7 5.5 %terms.1 = bf16[32,1,16,128]{3,2,1,0:T(8,128)(2,1)} custom-call(s32[2]{0:T(128)} %pad_add_fusion.place_ref, s32[2]{0:T(128)} %valid_ref.1, s32[2,64]{1,0:T(2,128)} %bitcast.11, bf16[2,64,128]{2,1,0:T(8,128)(2,1)} %bitcast.10, bf16[2,64,128]{2,1,0:T(8,128)(2,1)} %copy-done, f32[96,4,128]{2,1,0:T(4,128)} %bitcast.7, f32[96,4,128]{2,1,0:T(4,128)} %bitcast.8), custom_call_target="tpu_custom_call" | custom-call | tf_op jit(solution)/shard_map/terms/pallas_call | solution.py:195
  11.2 14.3 %all_to_all.5.got_ref = bf16[32,1,16,128]{3,2,1,0:T(8,128)(2,1)} all-to-all(bf16[32,1,16,128]{3,2,1,0:T(8,128)(2,1)} %terms.1), channel_id=1, replica_groups=mesh['det'=4,'tm'=8] {'det','tm'}, dimensions={0} | all-to-all | bytes 262144 | tf_op jit(solution)/shard_map/all_to_all | solution.py:211
  25.5 1.5 %sum.1 = f32[12,128]{1,0:T(8,128)} custom-call(bf16[32,1,16,128]{3,2,1,0:T(8,128)(2,1)} %all_to_all.5.got_ref), custom_call_target="tpu_custom_call" | custom-call | tf_op jit(solution)/shard_map/sum/pallas_call | solution.py:212
Async XLA Ops:
  0.0 5.1 %collective-permute-start = (bf16[2,64,128]{2,1,0:T(8,128)(2,1)}, bf16[2,64,128]{2,1,0:T(8,128)(2,1)S(1)}, u32[]{:S(2)}, u32[]{:S(2)}) collective-permute-start(bf16[2,64,128]{2,1,0:T(8,128)(2,1)} %bitcast.9), channel_id=1, source_target_pairs={{0,16},{8,24},{16,0},{24,8},{1,17},{9,25},{17,1},{25,9},{2,18},{10... | collective-permute-start | bytes 98312 | tf_op jit(solution)/shard_map/ppermute | solution.py:193
  5.1 0.6 %copy-start = (bf16[2,64,128]{2,1,0:T(8,128)(2,1)}, bf16[2,64,128]{2,1,0:T(8,128)(2,1)S(1)}, u32[]{:S(2)}) copy-start(bf16[2,64,128]{2,1,0:T(8,128)(2,1)S(1)} %collective-permute-done.other_ref) | copy-start | bytes 98308

commit v2 on v1

--- a/solution.py
+++ b/solution.py
@@ -14,11 +14,13 @@
 LANES = 128
 INNER = 16
 PARTS = 6
+UNROLLED = 16
+GRANT = pltpu.CompilerParams(vmem_limit_bytes=8 << 20)
 
 NEAR_COS = (0.9999999994443334, -19.739207715972064, 64.93905415215964, -85.41956519425082, 58.57456432893444)
 NEAR_SIN = (6.283185306861161, -41.341701618023556, 81.60505457483515, -76.68452620857785, 41.10289536853278)
 VMEM = pl.BlockSpec(memory_space=pltpu.VMEM)
-SMEM = pl.BlockSpec(memory_space=pltpu.SMEM)
+HBM = pl.BlockSpec(memory_space=pltpu.HBM)
 
 
 def fitted(function, limit, degree):
@@ -55,23 +57,108 @@
     return high, (x - high.astype(jnp.float32)).astype(jnp.bfloat16)
 
 
-def terms_kernel(
-    tm_count, rows_dest, seg_kept,
-    place_ref, valid_ref, table_ref, own_ref, other_ref, lags_ref, drift_ref,
-    out_ref,
-    own32, other32, cross, masked, left, total,
+def block_of(slot, table_ref, tm_count, bin_half):
+    per_group = table_ref.shape[1] // (2 * tm_count)
+    first = slot * TPB
+    return (2 * (first // per_group) + bin_half) * per_group + first % per_group
+
+
+def over_slots(slots, one_slot):
+    if slots <= UNROLLED:
+        for slot in range(slots):
+            one_slot(slot)
+    else:
+        lax.fori_loop(0, slots, lambda slot, _: (one_slot(slot), 0)[1], 0)
+
+
+def inner_tables(tile, lags_ref, inner_at):
+    lag = jnp.concatenate([lags_ref[tile, c : c + 1, :] for c in range(PT // LANES)], 1)
+    cosine, sine = near_turn(jnp.broadcast_to(lag, inner_at.shape) * inner_at)
+    cos_high, cos_low = split(cosine)
+    sin_high, sin_low = split(sine)
+    return lag, (cos_high, sin_high, cos_low, sin_low)
+
+
+def outer_tables(tile, lag, drift_ref, turn, frequency, live):
+    pace = jnp.concatenate([drift_ref[tile, c : c + 1, :] for c in range(PT // LANES)], 1)
+    shape = frequency.shape
+    cosine, sine = any_turn(jnp.broadcast_to(pace * turn, shape) - frequency * jnp.broadcast_to(lag, shape))
+    return cosine * live, sine * live
+
+
+def clock(valid_ref, tm_count, detector_bit, seg_kept):
+    tm_index = lax.axis_index("tm")
+    seg_count = valid_ref.shape[0]
+    segment_total = seg_count * tm_count
+    marks = []
+    for s in range(seg_kept):
+        seg = detector_bit * seg_kept + s
+        time = ((tm_index * seg_count + seg).astype(jnp.float32) + 0.5 - segment_total / 2) / segment_total
+        marks.append((valid_ref[seg].astype(jnp.float32), time))
+    return marks
+
+
+def fetch(sources, targets, sems):
+    copies = [pltpu.make_async_copy(a, b, sems.at[n]) for n, (a, b) in enumerate(zip(sources, targets))]
+    for copy in copies:
+        copy.start()
+    return copies
+
+
+def start_rows(outer):
+    return (lax.broadcasted_iota(jnp.int32, (outer, PT), 0) * INNER).astype(jnp.float32)
+
+
+def inner_rows():
+    return lax.broadcasted_iota(jnp.int32, (INNER, PT), 0).astype(jnp.float32)
+
+
+def tables_kernel(
+    tm_count, bands_half, width, seg_kept,
+    valid_hbm, table_hbm, lags_hbm, drift_hbm,
+    inner_ref, outer_ref,
+    valid_ref, table_ref, lags_ref, drift_ref, sems,
 ):
-    det_index, tm_index = place_ref[0], place_ref[1]
-    bin_half = det_index % 2
-    detector_bit = det_index // 2
+    det_index = lax.axis_index("det")
+    bin_half, detector_bit = det_index % 2, det_index // 2
+    copies = fetch((valid_hbm, table_hbm, lags_hbm, drift_hbm), (valid_ref, table_ref, lags_ref, drift_ref), sems)
+    inner_at, start_at = inner_rows(), start_rows(width // INNER)
+    for copy in copies:
+        copy.wait()
+    marks = clock(valid_ref, tm_count, detector_bit, seg_kept)
+
+    def one_slot(slot):
+        row = block_of(slot, table_ref, tm_count, bin_half)
+        band = table_ref[0, row]
+        frequency = (band * width).astype(jnp.float32) + start_at
+        share = (band.astype(jnp.float32) + 0.5) / (2 * bands_half)
+        for m in range(TPB):
+            tile = table_ref[1, row + m]
+            at = slot * TPB + m
+            lag, parts = inner_tables(tile, lags_ref, inner_at)
+            inner_ref[at] = jnp.concatenate(parts, 0)
+            for s, (live, time) in enumerate(marks):
+                cosine, sine = outer_tables(tile, lag, drift_ref, share * time, frequency, live)
+                outer_ref[at, s, 0] = cosine
+                outer_ref[at, s, 1] = sine
+
+    over_slots(inner_ref.shape[0] // TPB, one_slot)
+
+
+def terms_kernel(tm_count, rows_dest, seg_kept, ready, *refs):
+    if ready:
+        table_hbm, inner_ref, outer_ref, own_ref, other_ref, out_ref, table_ref, sems, *scratch = refs
+        copies = fetch((table_hbm,), (table_ref,), sems)
+    else:
+        valid_hbm, table_hbm, lags_hbm, drift_hbm, own_ref, other_ref, out_ref, *scratch = refs
+        valid_ref, table_ref, lags_ref, drift_ref, sems, *scratch = scratch
+        copies = fetch((valid_hbm, table_hbm, lags_hbm, drift_hbm), (valid_ref, table_ref, lags_ref, drift_ref), sems)
+    own32, other32, cross, masked, left, total = scratch
+    det_index = lax.axis_index("det")
+    bin_half, detector_bit = det_index % 2, det_index // 2
     bands_half = own_ref.shape[1] // 2
     width = own_ref.shape[2]
     outer = width // INNER
-    seg_count = own_ref.shape[0]
-    segment_total = seg_count * tm_count
-    band_total = 2 * bands_half
-    per_group = table_ref.shape[1] // (2 * tm_count)
-    slots = tm_count * per_group // TPB
     per_tile = PT // LANES
     flip = jnp.where(detector_bit == 0, 1.0, -1.0).astype(jnp.float32)
     outer_at = lax.broadcasted_iota(jnp.int32, (outer, width), 0)
@@ -89,8 +176,6 @@
         return (same & chosen).astype(jnp.float32).astype(jnp.bfloat16)
 
     choose = jnp.concatenate([chooser(0, 4), chooser(1, 5), chooser(2), chooser(3)], 0)
-    inner_at = lax.broadcasted_iota(jnp.int32, (INNER, PT), 0).astype(jnp.float32)
-    start_at = (lax.broadcasted_iota(jnp.int32, (outer, PT), 0) * INNER).astype(jnp.float32)
     total[...] = jnp.zeros_like(total)
 
     for s in range(seg_kept):
@@ -115,35 +200,38 @@
             .astype(jnp.bfloat16)
             .reshape(bands_half, 2 * outer, LANES)
         )
-        time_coord = ((tm_index * seg_count + seg).astype(jnp.float32) + 0.5 - segment_total / 2) / segment_total
-        live = valid_ref[seg].astype(jnp.float32)
-
-        def one_slot(slot, _):
-            group = slot * TPB // per_group
-            row = (2 * group + bin_half) * per_group + slot * TPB % per_group
+        if s == 0:
+            for copy in copies:
+                copy.wait()
+        if not ready:
+            inner_at, start_at = inner_rows(), start_rows(outer)
+            live, time = clock(valid_ref, tm_count, detector_bit, seg_kept)[s]
+
+        def one_slot(slot):
+            row = block_of(slot, table_ref, tm_count, bin_half)
             band = table_ref[0, row]
             lhs = left[band - bin_half * bands_half][:, : PARTS * INNER]
-            turn = (band.astype(jnp.float32) + 0.5) / band_total * time_coord
-            frequency = (band * width).astype(jnp.float32) + start_at
             for m in range(TPB):
+                at = slot * TPB + m
                 tile = table_ref[1, row + m]
-                lag = jnp.concatenate([lags_ref[tile, c : c + 1, :] for c in range(per_tile)], 1)
-                pace = jnp.concatenate([drift_ref[tile, c : c + 1, :] for c in range(per_tile)], 1)
-                cosine, sine = near_turn(jnp.broadcast_to(lag, (INNER, PT)) * inner_at)
-                cos_high, cos_low = split(cosine)
-                sin_high, sin_low = split(sine)
-                rhs = jnp.concatenate([cos_high, sin_high, cos_high, sin_high, cos_low, sin_low], 0)
+                if ready:
+                    table = inner_ref[at]
+                    cosine, sine = outer_ref[at, s, 0], outer_ref[at, s, 1]
+                else:
+                    lag, parts = inner_tables(tile, lags_ref, inner_at)
+                    table = jnp.concatenate(parts, 0)
+                    turn = (band.astype(jnp.float32) + 0.5) / (2 * bands_half) * time
+                    frequency = (band * width).astype(jnp.float32) + start_at
+                    cosine, sine = outer_tables(tile, lag, drift_ref, turn, frequency, live)
+                rhs = jnp.concatenate([table[: 2 * INNER], table], 0)
                 product = jnp.dot(lhs, rhs, preferred_element_type=jnp.float32)
-                angle = jnp.broadcast_to(pace * turn, (outer, PT)) - frequency * jnp.broadcast_to(lag, (outer, PT))
-                cosine, sine = any_turn(angle)
-                terms = jnp.sum(cosine * product[:outer] - sine * product[outer:], axis=0, keepdims=True) * live
+                terms = jnp.sum(cosine * product[:outer] - sine * product[outer:], axis=0, keepdims=True)
                 for c in range(per_tile):
-                    at = tile * per_tile + c
-                    where = at // rows_dest, s, pl.ds(at % rows_dest, 1)
+                    piece = tile * per_tile + c
+                    where = piece // rows_dest, s, pl.ds(piece % rows_dest, 1)
                     total[where] += terms[:, c * LANES : (c + 1) * LANES]
-            return 0
-
-        lax.fori_loop(0, slots, one_slot, 0)
+
+        over_slots(table_ref.shape[1] // 2 // TPB, one_slot)
         for n, data in enumerate((own32, other32)):
             power = jnp.sum(jnp.sum(data[...] * data[...], axis=0, keepdims=True), axis=1, keepdims=True)
             high = power.astype(jnp.bfloat16).astype(jnp.float32)
@@ -189,24 +277,51 @@
     rows = -(-(rows_dest + 4) // 8) * 8
     per_tile = PT // LANES
 
+    blocks = block_table.shape[0] // 2
+    outer = width // INNER
     own = own.reshape(seg_count, 2 * bands_half, width)
     other = lax.ppermute(own, "det", [(d, d ^ 2) for d in range(det_count)])
-    place = jnp.stack([lax.axis_index("det"), lax.axis_index("tm")]).astype(jnp.int32)
+    table = block_table.T
+    lags, drift = (x.reshape(-1, per_tile, LANES) for x in (lags, drift))
+    settings = tuple(pltpu.with_memory_space_constraint(x, pltpu.HBM) for x in (valid, table, lags, drift))
+    held = [pltpu.SMEM(valid.shape, jnp.int32), pltpu.SMEM(table.shape, jnp.int32)]
+    held += [pltpu.VMEM(lags.shape, jnp.float32), pltpu.VMEM(drift.shape, jnp.float32)]
+    held += [pltpu.SemaphoreType.DMA((len(settings),))]
+    tables = [
+        jax.ShapeDtypeStruct((blocks, 4 * INNER, PT), jnp.bfloat16),
+        jax.ShapeDtypeStruct((blocks, seg_kept, 2, outer, PT), jnp.float32),
+    ]
+    ready = blocks <= 4 * UNROLLED
+    if ready:
+        made = pl.pallas_call(
+            functools.partial(tables_kernel, tm_count, bands_half, width, seg_kept),
+            out_shape=tables,
+            in_specs=[HBM] * 4,
+            out_specs=[VMEM] * 2,
+            scratch_shapes=held,
+            compiler_params=GRANT,
+            cost_estimate=pl.CostEstimate(flops=10**9, bytes_accessed=10**6, transcendentals=0),
+            name="tables",
+        )(*settings)
+        settings = (table, *made)
+        held = [pltpu.SMEM(table.shape, jnp.int32), pltpu.SemaphoreType.DMA((1,))]
     outgoing = pl.pallas_call(
-        functools.partial(terms_kernel, tm_count, rows_dest, seg_kept),
+        functools.partial(terms_kernel, tm_count, rows_dest, seg_kept, ready),
         out_shape=jax.ShapeDtypeStruct((dests, seg_kept, rows, LANES), jnp.bfloat16),
-        in_specs=[SMEM] * 3 + [VMEM] * 4,
+        in_specs=([HBM] + [VMEM] * 2 if ready else [HBM] * 4) + [VMEM] * 2,
         out_specs=VMEM,
-        scratch_shapes=[
+        scratch_shapes=held
+        + [
             pltpu.VMEM((2 * bands_half, width), jnp.float32),
             pltpu.VMEM((2 * bands_half, width), jnp.float32),
             pltpu.VMEM((2, bands_half, width), jnp.float32),
-            pltpu.VMEM((bands_half, 2 * width // INNER, 4 * width), jnp.bfloat16),
-            pltpu.VMEM((bands_half, 2 * width // INNER, LANES), jnp.bfloat16),
+            pltpu.VMEM((bands_half, 2 * outer, 4 * width), jnp.bfloat16),
+            pltpu.VMEM((bands_half, 2 * outer, LANES), jnp.bfloat16),
             pltpu.VMEM((dests, seg_kept, rows, LANES), jnp.float32),
         ],
+        compiler_params=GRANT,
         name="terms",
-    )(place, valid, block_table.T, own, other, lags.reshape(-1, per_tile, LANES), drift.reshape(-1, per_tile, LANES))
+    )(*settings, own, other)
     if direct:
         received = lax.all_to_all(outgoing, ("det", "tm"), 0, 0, tiled=True)
         result = pl.pallas_call(
@@ -214,6 +329,7 @@
             out_shape=jax.ShapeDtypeStruct((rows_dest, LANES), jnp.float32),
             in_specs=[VMEM],
             out_specs=VMEM,
+            compiler_params=GRANT,
             name="sum",
         )(received)
         return result.reshape(-1)

time: 27.2 us -> 21.6 us (0.79)
  Pallas kernels: 7.04 us -> 4.95 us
  waiting for transfers between devices: 1.45 us -> 0.01 us
  blocking collectives: 14.3 us -> 13.5 us
  other arithmetic: 0.65 us -> 0 us
  local copies, waits for them, and re-layouts: 0.61 us -> 0.01 us
    pallas_call x1, Pallas kernels: 5.5 us -> 1.75 us  [shards(): pl.pallas_call(functools.partial(terms_kernel, tm_count, rows_dest, seg_k...]
    pallas_call x0 -> x1, Pallas kernels: none -> 2.56 us  [shards(): pl.pallas_call(functools.partial(tables_kernel, tm_count, bands_half, wid...]
    ppermute x1, waiting for transfers between devices: 1.45 us -> 0.01 us  [shards(): other = lax.ppermute(own, 'det', [(d, d ^ 2) for d in range(det_count)])]
    pallas_call x1, Pallas kernels: 1.55 us -> 0.65 us  [shards(): pl.pallas_call(functools.partial(sum_kernel, tm_count, rows_dest, fourier...]
    all_to_all x1, blocking collectives: 14.3 us -> 13.5 us  [shards(): received = lax.all_to_all(outgoing, ('det', 'tm'), 0, 0, tiled=True)]
    another operation x1 -> x0, other arithmetic: 0.65 us -> none  [shards(): jnp.stack([lax.axis_index('det'), lax.axis_index('tm')]).astype(jnp.int32)]
    unnamed x2 -> x4, local copies, waits for them, and re-layouts: 0.61 us -> 0.01 us
  transfers between devices with their start and end apart: 1 -> 1, of which waited for: 1 -> 0; matrix products, arithmetic and copies ran while one was open for 2% -> 0% of each run, Pallas kernels for 0% -> 12%
where the time goes in v2:
time: 21.6 us; the launch traced here: 21.5 us
  blocking collectives  13.5 us (62%)
  Pallas kernels  4.95 us (23%)
  starting transfers between devices  3 us (14%)
    all_to_all x1, blocking collectives, shards(): received = lax.all_to_all(outgoing, ('det', 'tm'), 0, 0, tiled=True)  13.5 us
    ppermute x1, starting transfers between devices, shards(): other = lax.ppermute(own, 'det', [(d, d ^ 2) for d in range(det_count)])  3 us
    pallas_call x1, Pallas kernels, shards(): pl.pallas_call(functools.partial(tables_kernel, tm_count, bands_half, wid...  2.56 us
    pallas_call x1, Pallas kernels, shards(): pl.pallas_call(functools.partial(terms_kernel, tm_count, rows_dest, seg_k...  1.75 us
    pallas_call x1, Pallas kernels, shards(): pl.pallas_call(functools.partial(sum_kernel, tm_count, rows_dest, fourier...  0.65 us
  transfers between devices with their start and end apart: 1, of which 0 were waited for; matrix products, arithmetic and copies ran while one was open for 0% of the time, Pallas kernels for 12%

profile of v2, /device:TPU:0, one launch (start us, length us, event | category | flops | bytes accessed | tf_op | source)
XLA Modules:
  0.0 21.5 jit_solution(14132678848706169944)
XLA Ops:
  0.0 0.0 copy-start
  0.0 0.0 copy-start.1
  0.0 3.0 %collective-permute-start = (bf16[2,64,128]{2,1,0:T(8,128)(2,1)}, bf16[2,64,128]{2,1,0:T(8,128)(2,1)S(1)}, u32[]{:S(2)}, u32[]{:S(2)}) collective-permute-start(bf16[2,64,128]{2,1,0:T(8,128)(2,1)} %bitcast.5), channel_id=1, source_target_pairs={{0,16},{8,24},{16,0},{24,8},{1,17},{9,25},{17,1},{25,9},{2,18},{10... | collective-permute-start | bytes 98312 | tf_op jit(solution)/shard_map/ppermute | solution.py:283
  3.0 2.6 %tables.1 = (bf16[32,64,512]{2,1,0:T(8,128)(2,1)S(1)}, f32[32,1,2,8,512]{4,3,2,1,0:T(8,128)S(1)}) custom-call(s32[2]{0:T(128)} %valid_hbm.1, s32[2,64]{1,0:T(2,128)} %bitcast.7, f32[96,4,128]{2,1,0:T(4,128)} %bitcast.9, f32[96,4,128]{2,1,0:T(4,128)} %bitcast.10), custom_call_target="tpu_custom_call" | custom-call | flops 1000000000 | bytes 1000000 | tf_op jit(solution)/shard_map/tables/pallas_call | solution.py:296
  5.6 0.0 collective-permute-done.refs_4_
  5.6 0.0 copy-done
  5.6 0.0 copy-done.1
  5.6 1.8 %terms.1 = bf16[32,1,16,128]{3,2,1,0:T(8,128)(2,1)S(1)} custom-call(s32[2,64]{1,0:T(2,128)S(1)} %bitcast.8, bf16[32,64,512]{2,1,0:T(8,128)(2,1)S(1)} %get-tuple-element.7.refs_1_, f32[32,1,2,8,512]{4,3,2,1,0:T(8,128)S(1)} %get-tuple-element.8.refs_2_, bf16[2,64,128]{2,1,0:T(8,128)(2,1)S(1)} %bitcast.6, bf16[2,64,128]{2,1,0:T(8,128)(2,1)S(1)} %collective-permute-done.refs_4_), custom_call_target="tpu_custom_call" | custom-call | tf_op jit(solution)/shard_map/terms/pallas_call | solution.py:308
  7.4 13.5 %all_to_all.5.got_ref = bf16[32,1,16,128]{3,2,1,0:T(8,128)(2,1)S(1)} all-to-all(bf16[32,1,16,128]{3,2,1,0:T(8,128)(2,1)S(1)} %terms.1), channel_id=1, replica_groups=mesh['det'=4,'tm'=8] {'det','tm'}, dimensions={0} | all-to-all | bytes 262144 | tf_op jit(solution)/shard_map/all_to_all | solution.py:326
  20.8 0.6 %sum.1 = f32[12,128]{1,0:T(8,128)} custom-call(bf16[32,1,16,128]{3,2,1,0:T(8,128)(2,1)S(1)} %all_to_all.5.got_ref), custom_call_target="tpu_custom_call" | custom-call | tf_op jit(solution)/shard_map/sum/pallas_call | solution.py:327
Async XLA Ops:
  0.0 5.6 %copy-start = (bf16[1,2,32,2,128]{4,3,2,1,0:T(2,128)(2,1)S(1)}, bf16[1,2,32,2,128]{4,3,2,1,0:T(2,128)(2,1)}, u32[]{:S(2)}) copy-start(bf16[1,2,32,2,128]{4,3,2,1,0:T(2,128)(2,1)} %param.5) | copy-start | bytes 98308
  0.0 5.6 %copy-start.1 = (s32[64,2]{0,1:T(2,128)S(1)}, s32[64,2]{0,1:T(2,128)}, u32[]{:S(2)}) copy-start(s32[64,2]{0,1:T(2,128)} %param.9) | copy-start | bytes 1540
  0.0 5.6 %collective-permute-start = (bf16[2,64,128]{2,1,0:T(8,128)(2,1)}, bf16[2,64,128]{2,1,0:T(8,128)(2,1)S(1)}, u32[]{:S(2)}, u32[]{:S(2)}) collective-permute-start(bf16[2,64,128]{2,1,0:T(8,128)(2,1)} %bitcast.5), channel_id=1, source_target_pairs={{0,16},{8,24},{16,0},{24,8},{1,17},{9,25},{17,1},{25,9},{2,18},{10... | collective-permute-start | bytes 98312 | tf_op jit(solution)/shard_map/ppermute | solution.py:283

commit v3 on v2

--- a/solution.py
+++ b/solution.py
@@ -113,18 +113,68 @@
     return lax.broadcasted_iota(jnp.int32, (INNER, PT), 0).astype(jnp.float32)
 
 
+def spreading(outer, width):
+    lane_at = lax.broadcasted_iota(jnp.int32, (outer, width), 1)
+    mask = (lane_at // INNER == lax.broadcasted_iota(jnp.int32, (outer, width), 0)).astype(jnp.float32)
+    from_lane = lax.broadcasted_iota(jnp.int32, (width, LANES), 0)
+    to_lane = lax.broadcasted_iota(jnp.int32, (width, LANES), 1)
+    choose = (from_lane % INNER == to_lane % INNER).astype(jnp.float32).astype(jnp.bfloat16)
+    return mask, choose
+
+
+def spread(rows_ref, band_of, masked, outer, width):
+    mask, choose = spreading(outer, width)
+
+    def one_slot(slot):
+        row = 2 * band_of(slot)
+        pair = [jnp.broadcast_to(rows_ref[pl.ds(row + c, 1), :], (outer, width)) * mask for c in range(2)]
+        masked[slot] = jnp.concatenate(pair, 0).astype(jnp.bfloat16)
+
+    slots = masked.shape[0]
+    over_slots(slots, one_slot)
+    stacked = masked[...].reshape(slots * 2 * outer, width)
+    return jnp.dot(stacked, choose, preferred_element_type=jnp.float32).reshape(slots, 2 * outer, LANES)
+
+
+def mix_own(rows_ref, band_of, masked, mixed_ref, s, flip, outer, width):
+    wide = spread(rows_ref, band_of, masked, outer, width)
+    real, imag = wide[:, :outer], wide[:, outer:]
+    even = lax.broadcasted_iota(jnp.int32, real.shape, 2) // INNER % 2 == 0
+    mixed_ref[s, 0] = jnp.where(even, real, -flip * imag)
+    mixed_ref[s, 1] = jnp.where(even, imag, flip * real)
+    mixed_ref[s, 2] = jnp.where(even, -flip * imag, -real)
+    mixed_ref[s, 3] = jnp.where(even, flip * real, -imag)
+
+
+def power_rows(rows):
+    power = jnp.sum(jnp.sum(rows * rows, axis=0, keepdims=True), axis=1, keepdims=True)
+    high = power.astype(jnp.bfloat16).astype(jnp.float32)
+    return jnp.concatenate([jnp.broadcast_to(x, (1, LANES)) for x in (high, power - high)], 0)
+
+
 def tables_kernel(
     tm_count, bands_half, width, seg_kept,
-    valid_hbm, table_hbm, lags_hbm, drift_hbm,
-    inner_ref, outer_ref,
-    valid_ref, table_ref, lags_ref, drift_ref, sems,
+    valid_hbm, table_hbm, lags_hbm, drift_hbm, own_ref,
+    inner_ref, outer_ref, mixed_ref, power_ref,
+    valid_ref, table_ref, lags_ref, drift_ref, sems, rows32, masked,
 ):
     det_index = lax.axis_index("det")
     bin_half, detector_bit = det_index % 2, det_index // 2
     copies = fetch((valid_hbm, table_hbm, lags_hbm, drift_hbm), (valid_ref, table_ref, lags_ref, drift_ref), sems)
-    inner_at, start_at = inner_rows(), start_rows(width // INNER)
-    for copy in copies:
-        copy.wait()
+    outer = width // INNER
+    inner_at, start_at = inner_rows(), start_rows(outer)
+    flip = jnp.where(detector_bit == 0, 1.0, -1.0).astype(jnp.float32)
+    copies[1].wait()
+
+    def band_of(slot):
+        return table_ref[0, block_of(slot, table_ref, tm_count, bin_half)] - bin_half * bands_half
+
+    for s in range(seg_kept):
+        rows32[...] = own_ref[detector_bit * seg_kept + s].astype(jnp.float32)
+        power_ref[s] = power_rows(rows32[...])
+        mix_own(rows32, band_of, masked, mixed_ref, s, flip, outer, width)
+    for n in (0, 2, 3):
+        copies[n].wait()
     marks = clock(valid_ref, tm_count, detector_bit, seg_kept)
 
     def one_slot(slot):
@@ -145,72 +195,52 @@
     over_slots(inner_ref.shape[0] // TPB, one_slot)
 
 
-def terms_kernel(tm_count, rows_dest, seg_kept, ready, *refs):
+def terms_kernel(tm_count, dests, rows_dest, seg_kept, ready, *refs):
     if ready:
-        table_hbm, inner_ref, outer_ref, own_ref, other_ref, out_ref, table_ref, sems, *scratch = refs
+        table_hbm, inner_ref, outer_ref, mixed_ref, power_ref, other_ref, out_ref, table_ref, sems, *scratch = refs
         copies = fetch((table_hbm,), (table_ref,), sems)
     else:
         valid_hbm, table_hbm, lags_hbm, drift_hbm, own_ref, other_ref, out_ref, *scratch = refs
-        valid_ref, table_ref, lags_ref, drift_ref, sems, *scratch = scratch
+        valid_ref, table_ref, lags_ref, drift_ref, sems, mixed_ref, *scratch = scratch
         copies = fetch((valid_hbm, table_hbm, lags_hbm, drift_hbm), (valid_ref, table_ref, lags_ref, drift_ref), sems)
-    own32, other32, cross, masked, left, total = scratch
+    rows32, masked, left, total = scratch
     det_index = lax.axis_index("det")
     bin_half, detector_bit = det_index % 2, det_index // 2
-    bands_half = own_ref.shape[1] // 2
-    width = own_ref.shape[2]
+    bands_half = other_ref.shape[1] // 2
+    width = other_ref.shape[2]
     outer = width // INNER
     per_tile = PT // LANES
+    slots = masked.shape[0]
     flip = jnp.where(detector_bit == 0, 1.0, -1.0).astype(jnp.float32)
-    outer_at = lax.broadcasted_iota(jnp.int32, (outer, width), 0)
-    lane_at = lax.broadcasted_iota(jnp.int32, (outer, width), 1)
-    mask = (lane_at // INNER == outer_at).astype(jnp.float32)
-    from_lane = lax.broadcasted_iota(jnp.int32, (width, LANES), 0) % INNER
-    to_lane = lax.broadcasted_iota(jnp.int32, (width, LANES), 1)
-    same = from_lane == to_lane % INNER
-    part = to_lane // INNER
-
-    def chooser(*parts):
-        chosen = part == parts[0]
-        for p in parts[1:]:
-            chosen = chosen | (part == p)
-        return (same & chosen).astype(jnp.float32).astype(jnp.bfloat16)
-
-    choose = jnp.concatenate([chooser(0, 4), chooser(1, 5), chooser(2), chooser(3)], 0)
+    part = lax.broadcasted_iota(jnp.int32, (slots, outer, LANES), 2) // INNER
     total[...] = jnp.zeros_like(total)
+
+    def band_of(slot):
+        return table_ref[0, block_of(slot, table_ref, tm_count, bin_half)] - bin_half * bands_half
 
     for s in range(seg_kept):
         seg = detector_bit * seg_kept + s
-        own32[...] = own_ref[seg].astype(jnp.float32)
-        other32[...] = other_ref[seg].astype(jnp.float32)
-        own_r = own32[pl.ds(0, bands_half, stride=2), :]
-        own_i = own32[pl.ds(1, bands_half, stride=2), :]
-        other_r = other32[pl.ds(0, bands_half, stride=2), :]
-        other_i = other32[pl.ds(1, bands_half, stride=2), :]
-        cross[0] = own_r * other_r + own_i * other_i
-        cross[1] = (own_r * other_i - own_i * other_r) * flip
-        for b in range(bands_half):
-            real = jnp.broadcast_to(cross[0, b : b + 1, :], (outer, width)) * mask
-            imag = jnp.broadcast_to(cross[1, b : b + 1, :], (outer, width)) * mask
-            high, low = split(jnp.concatenate([real, imag], 0))
-            high_t, low_t = split(jnp.concatenate([imag, -real], 0))
-            masked[b] = jnp.concatenate([high, high_t, low, low_t], 1)
-        stacked = masked[...].reshape(bands_half * 2 * outer, 4 * width)
-        left[...] = (
-            jnp.dot(stacked, choose, preferred_element_type=jnp.float32)
-            .astype(jnp.bfloat16)
-            .reshape(bands_half, 2 * outer, LANES)
-        )
+        rows32[...] = other_ref[seg].astype(jnp.float32)
+        powers = [power_ref[s] if ready else power_rows(own_ref[seg].astype(jnp.float32)), power_rows(rows32[...])]
         if s == 0:
             for copy in copies:
                 copy.wait()
+        wide = spread(rows32, band_of, masked, outer, width)
         if not ready:
+            rows32[...] = own_ref[seg].astype(jnp.float32)
+            mix_own(rows32, band_of, masked, mixed_ref, s, flip, outer, width)
             inner_at, start_at = inner_rows(), start_rows(outer)
             live, time = clock(valid_ref, tm_count, detector_bit, seg_kept)[s]
+        real, imag = wide[:, :outer], wide[:, outer:]
+        for n in range(2):
+            value = mixed_ref[s, 2 * n] * real + mixed_ref[s, 2 * n + 1] * imag
+            high = value.astype(jnp.bfloat16).astype(jnp.float32)
+            parts = jnp.where((part == 2) | (part == 3), value - high, high)
+            left[:, n * outer : (n + 1) * outer, :] = parts
 
         def one_slot(slot):
             row = block_of(slot, table_ref, tm_count, bin_half)
-            band = table_ref[0, row]
-            lhs = left[band - bin_half * bands_half][:, : PARTS * INNER]
+            lhs = left[slot][:, : PARTS * INNER].astype(jnp.bfloat16)
             for m in range(TPB):
                 at = slot * TPB + m
                 tile = table_ref[1, row + m]
@@ -218,6 +248,7 @@
                     table = inner_ref[at]
                     cosine, sine = outer_ref[at, s, 0], outer_ref[at, s, 1]
                 else:
+                    band = table_ref[0, row]
                     lag, parts = inner_tables(tile, lags_ref, inner_at)
                     table = jnp.concatenate(parts, 0)
                     turn = (band.astype(jnp.float32) + 0.5) / (2 * bands_half) * time
@@ -226,19 +257,14 @@
                 rhs = jnp.concatenate([table[: 2 * INNER], table], 0)
                 product = jnp.dot(lhs, rhs, preferred_element_type=jnp.float32)
                 terms = jnp.sum(cosine * product[:outer] - sine * product[outer:], axis=0, keepdims=True)
-                for c in range(per_tile):
-                    piece = tile * per_tile + c
-                    where = piece // rows_dest, s, pl.ds(piece % rows_dest, 1)
-                    total[where] += terms[:, c * LANES : (c + 1) * LANES]
-
-        over_slots(table_ref.shape[1] // 2 // TPB, one_slot)
-        for n, data in enumerate((own32, other32)):
-            power = jnp.sum(jnp.sum(data[...] * data[...], axis=0, keepdims=True), axis=1, keepdims=True)
-            high = power.astype(jnp.bfloat16).astype(jnp.float32)
-            for p, value in enumerate((high, power - high)):
-                where = slice(None), s, pl.ds(rows_dest + 2 * n + p, 1)
-                total[where] = jnp.broadcast_to(value.reshape(1, 1, 1), (total.shape[0], 1, LANES))
-    out_ref[...] = total[...].astype(jnp.bfloat16)
+                total[s, tile] += jnp.concatenate([terms[:, c * LANES : (c + 1) * LANES] for c in range(per_tile)], 0)
+
+        over_slots(slots, one_slot)
+        tiles = rows_dest // per_tile
+        powers = jnp.concatenate(powers, 0)
+        for d in range(dests):
+            piece = total[s, d * tiles : (d + 1) * tiles].reshape(rows_dest, LANES)
+            out_ref[d, s] = jnp.concatenate([piece, powers], 0).astype(jnp.bfloat16)
 
 
 def weights_of(power, fourier_bins):
@@ -271,14 +297,15 @@
     per_device = pixels // devices
     fourier_bins = 2 * bands_half * width
     scale = math.sqrt(seg_count * tm_count * width)
-    direct = per_device % LANES == 0
+    direct = per_device % PT == 0
     rows_dest = (per_device if direct else pixels) // LANES
     dests = devices if direct else 1
-    rows = -(-(rows_dest + 4) // 8) * 8
+    rows = rows_dest + 4
     per_tile = PT // LANES
-
     blocks = block_table.shape[0] // 2
+    slots = blocks // TPB
     outer = width // INNER
+
     own = own.reshape(seg_count, 2 * bands_half, width)
     other = lax.ppermute(own, "det", [(d, d ^ 2) for d in range(det_count)])
     table = block_table.T
@@ -287,41 +314,44 @@
     held = [pltpu.SMEM(valid.shape, jnp.int32), pltpu.SMEM(table.shape, jnp.int32)]
     held += [pltpu.VMEM(lags.shape, jnp.float32), pltpu.VMEM(drift.shape, jnp.float32)]
     held += [pltpu.SemaphoreType.DMA((len(settings),))]
-    tables = [
-        jax.ShapeDtypeStruct((blocks, 4 * INNER, PT), jnp.bfloat16),
-        jax.ShapeDtypeStruct((blocks, seg_kept, 2, outer, PT), jnp.float32),
-    ]
-    ready = blocks <= 4 * UNROLLED
+    work = [pltpu.VMEM(own.shape[1:], jnp.float32), pltpu.VMEM((slots, 2 * outer, width), jnp.bfloat16)]
+    mixed = jax.ShapeDtypeStruct((seg_kept, 4, slots, outer, LANES), jnp.float32)
+    ready = slots <= UNROLLED
     if ready:
         made = pl.pallas_call(
             functools.partial(tables_kernel, tm_count, bands_half, width, seg_kept),
-            out_shape=tables,
-            in_specs=[HBM] * 4,
-            out_specs=[VMEM] * 2,
-            scratch_shapes=held,
+            out_shape=[
+                jax.ShapeDtypeStruct((blocks, 4 * INNER, PT), jnp.bfloat16),
+                jax.ShapeDtypeStruct((blocks, seg_kept, 2, outer, PT), jnp.float32),
+                mixed,
+                jax.ShapeDtypeStruct((seg_kept, 2, LANES), jnp.float32),
+            ],
+            in_specs=[HBM] * 4 + [VMEM],
+            out_specs=[VMEM] * 4,
+            scratch_shapes=held + work,
             compiler_params=GRANT,
             cost_estimate=pl.CostEstimate(flops=10**9, bytes_accessed=10**6, transcendentals=0),
             name="tables",
-        )(*settings)
+        )(*settings, own)
         settings = (table, *made)
         held = [pltpu.SMEM(table.shape, jnp.int32), pltpu.SemaphoreType.DMA((1,))]
+    else:
+        settings = (*settings, own)
+        held += [pltpu.VMEM(mixed.shape, mixed.dtype)]
     outgoing = pl.pallas_call(
-        functools.partial(terms_kernel, tm_count, rows_dest, seg_kept, ready),
+        functools.partial(terms_kernel, tm_count, dests, rows_dest, seg_kept, ready),
         out_shape=jax.ShapeDtypeStruct((dests, seg_kept, rows, LANES), jnp.bfloat16),
-        in_specs=([HBM] + [VMEM] * 2 if ready else [HBM] * 4) + [VMEM] * 2,
+        in_specs=([HBM] + [VMEM] * 4 if ready else [HBM] * 4 + [VMEM]) + [VMEM],
         out_specs=VMEM,
-        scratch_shapes=held
-        + [
-            pltpu.VMEM((2 * bands_half, width), jnp.float32),
-            pltpu.VMEM((2 * bands_half, width), jnp.float32),
-            pltpu.VMEM((2, bands_half, width), jnp.float32),
-            pltpu.VMEM((bands_half, 2 * outer, 4 * width), jnp.bfloat16),
-            pltpu.VMEM((bands_half, 2 * outer, LANES), jnp.bfloat16),
-            pltpu.VMEM((dests, seg_kept, rows, LANES), jnp.float32),
+        scratch_shapes=[
+            *held,
+            *work,
+            pltpu.VMEM((slots, 2 * outer, LANES), jnp.float32),
+            pltpu.VMEM((seg_kept, pixels // PT, per_tile, LANES), jnp.float32),
         ],
-        compiler_params=GRANT,
+        compiler_params=GRANT if ready else None,
         name="terms",
-    )(*settings, own, other)
+    )(*settings, other)
     if direct:
         received = lax.all_to_all(outgoing, ("det", "tm"), 0, 0, tiled=True)
         result = pl.pallas_call(

time: 21.6 us -> 21.2 us (0.981)
  blocking collectives: 13.5 us -> 12.7 us
  local copies, waits for them, and re-layouts: 0.01 us -> 0.79 us
  Pallas kernels: 4.95 us -> 4.48 us
    unnamed x4, local copies, waits for them, and re-layouts: 0.01 us -> 0.79 us
    all_to_all x1, blocking collectives: 13.5 us -> 12.7 us  [shards(): received = lax.all_to_all(outgoing, ('det', 'tm'), 0, 0, tiled=True)]
    pallas_call x1, Pallas kernels: 1.75 us -> 1.28 us  [shards(): pl.pallas_call(functools.partial(terms_kernel, tm_count, dests, rows_dest...]
where the time goes in v3:
time: 21.2 us; the launch traced here: 21 us
  blocking collectives  12.7 us (60%)
  Pallas kernels  4.48 us (21%)
  starting transfers between devices  3 us (14%)
  local copies, waits for them, and re-layouts  0.79 us (4%)
    all_to_all x1, blocking collectives, shards(): received = lax.all_to_all(outgoing, ('det', 'tm'), 0, 0, tiled=True)  12.7 us
    ppermute x1, starting transfers between devices, shards(): other = lax.ppermute(own, 'det', [(d, d ^ 2) for d in range(det_count)])  3 us
    pallas_call x1, Pallas kernels, shards(): pl.pallas_call(functools.partial(tables_kernel, tm_count, bands_half, wid...  2.56 us
    pallas_call x1, Pallas kernels, shards(): pl.pallas_call(functools.partial(terms_kernel, tm_count, dests, rows_dest...  1.28 us
    unnamed x4, local copies, waits for them, and re-layouts  0.79 us
    pallas_call x1, Pallas kernels, shards(): pl.pallas_call(functools.partial(sum_kernel, tm_count, rows_dest, fourier...  0.65 us
  transfers between devices with their start and end apart: 1, of which 0 were waited for; matrix products, arithmetic and copies ran while one was open for 0% of the time, Pallas kernels for 12%

profile of v3, /device:TPU:0, one launch (start us, length us, event | category | flops | bytes accessed | tf_op | source)
XLA Modules:
  0.0 21.0 jit_solution(6997250179567012734)
XLA Ops:
  0.0 0.0 copy-start
  0.0 3.0 %collective-permute-start = (bf16[2,64,128]{2,1,0:T(8,128)(2,1)}, bf16[2,64,128]{2,1,0:T(8,128)(2,1)S(1)}, u32[]{:S(2)}, u32[]{:S(2)}) collective-permute-start(bf16[2,64,128]{2,1,0:T(8,128)(2,1)} %bitcast.7), channel_id=1, source_target_pairs={{0,16},{8,24},{16,0},{24,8},{1,17},{9,25},{17,1},{25,9},{2,18},{10... | collective-permute-start | bytes 98312 | tf_op jit(solution)/shard_map/ppermute | solution.py:310
  3.0 0.0 copy-start.1
  3.0 0.8 %copy-done.1 = bf16[1,2,32,2,128]{4,3,2,1,0:T(2,128)(2,1)S(1)} copy-done((bf16[1,2,32,2,128]{4,3,2,1,0:T(2,128)(2,1)S(1)}, bf16[1,2,32,2,128]{4,3,2,1,0:T(2,128)(2,1)}, u32[]{:S(2)}) %copy-start.1) | copy-done | bytes 32792
  3.8 2.6 %tables.1 = (bf16[32,64,512]{2,1,0:T(8,128)(2,1)S(1)}, f32[32,1,2,8,512]{4,3,2,1,0:T(8,128)S(1)}, f32[1,4,16,8,128]{4,3,2,1,0:T(8,128)S(1)}, f32[1,2,128]{2,1,0:T(2,128)S(1)}) custom-call(s32[2]{0:T(128)} %valid_hbm.1, s32[2,64]{1,0:T(2,128)} %bitcast.5, f32[96,4,128]{2,1,0:T(4,128)} %bitcast.9, f32[96,4,128]{2,1,0:T(4,128)} %bitcast.10, ...), custom_call_target="tpu_custom_call" | custom-call | flops 1000000000 | bytes 1000000 | tf_op jit(solution)/shard_map/tables/pallas_call | solution.py:321
  6.4 0.0 collective-permute-done.refs_5_
  6.4 0.0 copy-done
  6.4 1.3 %terms.1 = bf16[32,1,16,128]{3,2,1,0:T(8,128)(2,1)S(1)} custom-call(s32[2,64]{1,0:T(2,128)S(1)} %bitcast.6, bf16[32,64,512]{2,1,0:T(8,128)(2,1)S(1)} %get-tuple-element.9.refs_1_, f32[32,1,2,8,512]{4,3,2,1,0:T(8,128)S(1)} %get-tuple-element.10.refs_2_, f32[1,4,16,8,128]{4,3,2,1,0:T(8,128)S(1)} %get-tuple-element.11.refs_3_, ...), custom_call_target="tpu_custom_call" | custom-call | tf_op jit(solution)/shard_map/terms/pallas_call | solution.py:341
  7.7 12.7 %all_to_all.5.got_ref = bf16[32,1,16,128]{3,2,1,0:T(8,128)(2,1)S(1)} all-to-all(bf16[32,1,16,128]{3,2,1,0:T(8,128)(2,1)S(1)} %terms.1), channel_id=1, replica_groups=mesh['det'=4,'tm'=8] {'det','tm'}, dimensions={0} | all-to-all | bytes 262144 | tf_op jit(solution)/shard_map/all_to_all | solution.py:356
  20.4 0.6 %sum.1 = f32[12,128]{1,0:T(8,128)} custom-call(bf16[32,1,16,128]{3,2,1,0:T(8,128)(2,1)S(1)} %all_to_all.5.got_ref), custom_call_target="tpu_custom_call" | custom-call | tf_op jit(solution)/shard_map/sum/pallas_call | solution.py:357
Async XLA Ops:
  0.0 6.4 %copy-start = (s32[64,2]{0,1:T(2,128)S(1)}, s32[64,2]{0,1:T(2,128)}, u32[]{:S(2)}) copy-start(s32[64,2]{0,1:T(2,128)} %param.9) | copy-start | bytes 1540
  0.0 6.4 %collective-permute-start = (bf16[2,64,128]{2,1,0:T(8,128)(2,1)}, bf16[2,64,128]{2,1,0:T(8,128)(2,1)S(1)}, u32[]{:S(2)}, u32[]{:S(2)}) collective-permute-start(bf16[2,64,128]{2,1,0:T(8,128)(2,1)} %bitcast.7), channel_id=1, source_target_pairs={{0,16},{8,24},{16,0},{24,8},{1,17},{9,25},{17,1},{25,9},{2,18},{10... | collective-permute-start | bytes 98312 | tf_op jit(solution)/shard_map/ppermute | solution.py:310
  3.0 0.8 %copy-start.1 = (bf16[1,2,32,2,128]{4,3,2,1,0:T(2,128)(2,1)S(1)}, bf16[1,2,32,2,128]{4,3,2,1,0:T(2,128)(2,1)}, u32[]{:S(2)}) copy-start(bf16[1,2,32,2,128]{4,3,2,1,0:T(2,128)(2,1)} %param.5) | copy-start | bytes 98308

commit v4 on v3

--- a/solution.py
+++ b/solution.py
@@ -154,16 +154,21 @@
 
 def tables_kernel(
     tm_count, bands_half, width, seg_kept,
-    valid_hbm, table_hbm, lags_hbm, drift_hbm, own_ref,
-    inner_ref, outer_ref, mixed_ref, power_ref,
-    valid_ref, table_ref, lags_ref, drift_ref, sems, rows32, masked,
+    valid_hbm, table_hbm, lags_hbm, drift_hbm, own_hbm,
+    inner_ref, outer_ref, mixed_ref, power_ref, picks_ref,
+    valid_ref, table_ref, lags_ref, drift_ref, own_ref, sems, rows32, masked,
 ):
     det_index = lax.axis_index("det")
     bin_half, detector_bit = det_index % 2, det_index // 2
-    copies = fetch((valid_hbm, table_hbm, lags_hbm, drift_hbm), (valid_ref, table_ref, lags_ref, drift_ref), sems)
+    copies = fetch(
+        (table_hbm, own_hbm, valid_hbm, lags_hbm, drift_hbm),
+        (table_ref, own_ref, valid_ref, lags_ref, drift_ref),
+        sems,
+    )
     outer = width // INNER
     inner_at, start_at = inner_rows(), start_rows(outer)
     flip = jnp.where(detector_bit == 0, 1.0, -1.0).astype(jnp.float32)
+    copies[0].wait()
     copies[1].wait()
 
     def band_of(slot):
@@ -173,8 +178,8 @@
         rows32[...] = own_ref[detector_bit * seg_kept + s].astype(jnp.float32)
         power_ref[s] = power_rows(rows32[...])
         mix_own(rows32, band_of, masked, mixed_ref, s, flip, outer, width)
-    for n in (0, 2, 3):
-        copies[n].wait()
+    for copy in copies[2:]:
+        copy.wait()
     marks = clock(valid_ref, tm_count, detector_bit, seg_kept)
 
     def one_slot(slot):
@@ -182,9 +187,11 @@
         band = table_ref[0, row]
         frequency = (band * width).astype(jnp.float32) + start_at
         share = (band.astype(jnp.float32) + 0.5) / (2 * bands_half)
+        picks_ref[slot : slot + 1, :] = jnp.full((1, LANES), band_of(slot))
         for m in range(TPB):
             tile = table_ref[1, row + m]
             at = slot * TPB + m
+            picks_ref[slots + at : slots + at + 1, :] = jnp.full((1, LANES), tile)
             lag, parts = inner_tables(tile, lags_ref, inner_at)
             inner_ref[at] = jnp.concatenate(parts, 0)
             for s, (live, time) in enumerate(marks):
@@ -192,13 +199,14 @@
                 outer_ref[at, s, 0] = cosine
                 outer_ref[at, s, 1] = sine
 
-    over_slots(inner_ref.shape[0] // TPB, one_slot)
+    slots = inner_ref.shape[0] // TPB
+    over_slots(slots, one_slot)
 
 
 def terms_kernel(tm_count, dests, rows_dest, seg_kept, ready, *refs):
     if ready:
-        table_hbm, inner_ref, outer_ref, mixed_ref, power_ref, other_ref, out_ref, table_ref, sems, *scratch = refs
-        copies = fetch((table_hbm,), (table_ref,), sems)
+        inner_ref, outer_ref, mixed_ref, power_ref, picks_ref, other_ref, out_ref, *scratch = refs
+        copies = ()
     else:
         valid_hbm, table_hbm, lags_hbm, drift_hbm, own_ref, other_ref, out_ref, *scratch = refs
         valid_ref, table_ref, lags_ref, drift_ref, sems, mixed_ref, *scratch = scratch
@@ -216,7 +224,14 @@
     total[...] = jnp.zeros_like(total)
 
     def band_of(slot):
+        if ready:
+            return picks_ref[slot : slot + 1, :][0, 0]
         return table_ref[0, block_of(slot, table_ref, tm_count, bin_half)] - bin_half * bands_half
+
+    def tile_of(at):
+        if ready:
+            return picks_ref[slots + at : slots + at + 1, :][0, 0]
+        return table_ref[1, block_of(at // TPB, table_ref, tm_count, bin_half) + at % TPB]
 
     for s in range(seg_kept):
         seg = detector_bit * seg_kept + s
@@ -239,16 +254,15 @@
             left[:, n * outer : (n + 1) * outer, :] = parts
 
         def one_slot(slot):
-            row = block_of(slot, table_ref, tm_count, bin_half)
             lhs = left[slot][:, : PARTS * INNER].astype(jnp.bfloat16)
             for m in range(TPB):
                 at = slot * TPB + m
-                tile = table_ref[1, row + m]
+                tile = tile_of(at)
                 if ready:
                     table = inner_ref[at]
                     cosine, sine = outer_ref[at, s, 0], outer_ref[at, s, 1]
                 else:
-                    band = table_ref[0, row]
+                    band = band_of(slot) + bin_half * bands_half
                     lag, parts = inner_tables(tile, lags_ref, inner_at)
                     table = jnp.concatenate(parts, 0)
                     turn = (band.astype(jnp.float32) + 0.5) / (2 * bands_half) * time
@@ -313,7 +327,6 @@
     settings = tuple(pltpu.with_memory_space_constraint(x, pltpu.HBM) for x in (valid, table, lags, drift))
     held = [pltpu.SMEM(valid.shape, jnp.int32), pltpu.SMEM(table.shape, jnp.int32)]
     held += [pltpu.VMEM(lags.shape, jnp.float32), pltpu.VMEM(drift.shape, jnp.float32)]
-    held += [pltpu.SemaphoreType.DMA((len(settings),))]
     work = [pltpu.VMEM(own.shape[1:], jnp.float32), pltpu.VMEM((slots, 2 * outer, width), jnp.bfloat16)]
     mixed = jax.ShapeDtypeStruct((seg_kept, 4, slots, outer, LANES), jnp.float32)
     ready = slots <= UNROLLED
@@ -325,23 +338,23 @@
                 jax.ShapeDtypeStruct((blocks, seg_kept, 2, outer, PT), jnp.float32),
                 mixed,
                 jax.ShapeDtypeStruct((seg_kept, 2, LANES), jnp.float32),
+                jax.ShapeDtypeStruct((slots + blocks, LANES), jnp.int32),
             ],
-            in_specs=[HBM] * 4 + [VMEM],
-            out_specs=[VMEM] * 4,
-            scratch_shapes=held + work,
+            in_specs=[HBM] * 5,
+            out_specs=[VMEM] * 5,
+            scratch_shapes=[*held, pltpu.VMEM(own.shape, own.dtype), pltpu.SemaphoreType.DMA((5,)), *work],
             compiler_params=GRANT,
             cost_estimate=pl.CostEstimate(flops=10**9, bytes_accessed=10**6, transcendentals=0),
             name="tables",
-        )(*settings, own)
-        settings = (table, *made)
-        held = [pltpu.SMEM(table.shape, jnp.int32), pltpu.SemaphoreType.DMA((1,))]
+        )(*settings, pltpu.with_memory_space_constraint(own, pltpu.HBM))
+        settings, held = made, []
     else:
         settings = (*settings, own)
-        held += [pltpu.VMEM(mixed.shape, mixed.dtype)]
+        held += [pltpu.SemaphoreType.DMA((4,)), pltpu.VMEM(mixed.shape, mixed.dtype)]
     outgoing = pl.pallas_call(
         functools.partial(terms_kernel, tm_count, dests, rows_dest, seg_kept, ready),
         out_shape=jax.ShapeDtypeStruct((dests, seg_kept, rows, LANES), jnp.bfloat16),
-        in_specs=([HBM] + [VMEM] * 4 if ready else [HBM] * 4 + [VMEM]) + [VMEM],
+        in_specs=([VMEM] * 5 if ready else [HBM] * 4 + [VMEM]) + [VMEM],
         out_specs=VMEM,
         scratch_shapes=[
             *held,

time: 21.2 us -> 20.7 us (0.976)
  blocking collectives: 12.7 us -> 13.5 us
  local copies, waits for them, and re-layouts: 0.79 us -> 0 us
  Pallas kernels: 4.48 us -> 4.06 us
    unnamed x4 -> x0, local copies, waits for them, and re-layouts: 0.79 us -> none
    all_to_all x1, blocking collectives: 12.7 us -> 13.5 us  [shards(): received = lax.all_to_all(outgoing, ('det', 'tm'), 0, 0, tiled=True)]
    pallas_call x1, Pallas kernels: 1.28 us -> 0.83 us  [shards(): pl.pallas_call(functools.partial(terms_kernel, tm_count, dests, rows_dest...]
  transfers between devices with their start and end apart: 1 -> 1, of which waited for: 0 -> 0; matrix products, arithmetic and copies ran while one was open for 0% -> 0% of each run, Pallas kernels for 12% -> 13%
where the time goes in v4:
time: 20.7 us; the launch traced here: 20.5 us
  blocking collectives  13.5 us (65%)
  Pallas kernels  4.06 us (20%)
  starting transfers between devices  3 us (14%)
    all_to_all x1, blocking collectives, shards(): received = lax.all_to_all(outgoing, ('det', 'tm'), 0, 0, tiled=True)  13.5 us
    ppermute x1, starting transfers between devices, shards(): other = lax.ppermute(own, 'det', [(d, d ^ 2) for d in range(det_count)])  3 us
    pallas_call x1, Pallas kernels, shards(): pl.pallas_call(functools.partial(tables_kernel, tm_count, bands_half, wid...  2.59 us
    pallas_call x1, Pallas kernels, shards(): pl.pallas_call(functools.partial(terms_kernel, tm_count, dests, rows_dest...  0.83 us
    pallas_call x1, Pallas kernels, shards(): pl.pallas_call(functools.partial(sum_kernel, tm_count, rows_dest, fourier...  0.65 us
  transfers between devices with their start and end apart: 1, of which 0 were waited for; matrix products, arithmetic and copies ran while one was open for 0% of the time, Pallas kernels for 13%

profile of v4, /device:TPU:0, one launch (start us, length us, event | category | flops | bytes accessed | tf_op | source)
XLA Modules:
  0.0 20.5 jit_solution(6693186891877774491)
XLA Ops:
  0.0 3.0 %collective-permute-start = (bf16[2,64,128]{2,1,0:T(8,128)(2,1)}, bf16[2,64,128]{2,1,0:T(8,128)(2,1)S(1)}, u32[]{:S(2)}, u32[]{:S(2)}) collective-permute-start(bf16[2,64,128]{2,1,0:T(8,128)(2,1)} %bitcast.7), channel_id=1, source_target_pairs={{0,16},{8,24},{16,0},{24,8},{1,17},{9,25},{17,1},{25,9},{2,18},{10... | collective-permute-start | bytes 98312 | tf_op jit(solution)/shard_map/ppermute | solution.py:324
  3.0 2.6 %tables.1 = (bf16[32,64,512]{2,1,0:T(8,128)(2,1)S(1)}, f32[32,1,2,8,512]{4,3,2,1,0:T(8,128)S(1)}, f32[1,4,16,8,128]{4,3,2,1,0:T(8,128)S(1)}, f32[1,2,128]{2,1,0:T(2,128)S(1)}, s32[48,128]{1,0:T(8,128)S(1)}) custom-call(s32[2]{0:T(128)} %valid_hbm.1, s32[2,64]{1,0:T(2,128)} %bitcast.9, f32[96,4,128]{2,1,0:T(4,128)} %bitcast.5, f32[96,4,128]{2,1,0:T(4,128)} %bitcast.6, ...), custom_call_target="tpu_custom_call" | custom-call | flops 1000000000 | bytes 1000000 | tf_op jit(solution)/shard_map/tables/pallas_call | solution.py:334
  5.6 0.0 collective-permute-done.refs_5_
  5.6 0.8 %terms.1 = bf16[32,1,16,128]{3,2,1,0:T(8,128)(2,1)S(1)} custom-call(bf16[32,64,512]{2,1,0:T(8,128)(2,1)S(1)} %get-tuple-element.10.refs_0_, f32[32,1,2,8,512]{4,3,2,1,0:T(8,128)S(1)} %get-tuple-element.11.refs_1_, f32[1,4,16,8,128]{4,3,2,1,0:T(8,128)S(1)} %get-tuple-element.12.refs_2_, f32[1,2,128]{2,1,0:T(2,128)S(1)} %get-tuple-element.13.refs_3_, ...), custom_call_target="tpu_custom_call" | custom-call | tf_op jit(solution)/shard_map/terms/pallas_call | solution.py:354
  6.4 13.5 %all_to_all.5.got_ref = bf16[32,1,16,128]{3,2,1,0:T(8,128)(2,1)S(1)} all-to-all(bf16[32,1,16,128]{3,2,1,0:T(8,128)(2,1)S(1)} %terms.1), channel_id=1, replica_groups=mesh['det'=4,'tm'=8] {'det','tm'}, dimensions={0} | all-to-all | bytes 262144 | tf_op jit(solution)/shard_map/all_to_all | solution.py:369
  19.9 0.6 %sum.1 = f32[12,128]{1,0:T(8,128)} custom-call(bf16[32,1,16,128]{3,2,1,0:T(8,128)(2,1)S(1)} %all_to_all.5.got_ref), custom_call_target="tpu_custom_call" | custom-call | tf_op jit(solution)/shard_map/sum/pallas_call | solution.py:370
Async XLA Ops:
  0.0 5.6 %collective-permute-start = (bf16[2,64,128]{2,1,0:T(8,128)(2,1)}, bf16[2,64,128]{2,1,0:T(8,128)(2,1)S(1)}, u32[]{:S(2)}, u32[]{:S(2)}) collective-permute-start(bf16[2,64,128]{2,1,0:T(8,128)(2,1)} %bitcast.7), channel_id=1, source_target_pairs={{0,16},{8,24},{16,0},{24,8},{1,17},{9,25},{17,1},{25,9},{2,18},{10... | collective-permute-start | bytes 98312 | tf_op jit(solution)/shard_map/ppermute | solution.py:324

commit v5 on v4

--- a/solution.py
+++ b/solution.py
@@ -13,12 +13,11 @@
 TPB = 2
 LANES = 128
 INNER = 16
+HALF = INNER // 2
 PARTS = 6
 UNROLLED = 16
 GRANT = pltpu.CompilerParams(vmem_limit_bytes=8 << 20)
 
-NEAR_COS = (0.9999999994443334, -19.739207715972064, 64.93905415215964, -85.41956519425082, 58.57456432893444)
-NEAR_SIN = (6.283185306861161, -41.341701618023556, 81.60505457483515, -76.68452620857785, 41.10289536853278)
 VMEM = pl.BlockSpec(memory_space=pltpu.VMEM)
 HBM = pl.BlockSpec(memory_space=pltpu.HBM)
 
@@ -30,6 +29,8 @@
     return tuple(float(c) for c in coefficients / limit ** np.arange(degree + 1))
 
 
+NEAR_COS = fitted(lambda r: np.cos(2 * np.pi * r), 0.0064, 3)
+NEAR_SIN = fitted(lambda r: np.sin(2 * np.pi * r) / r, 0.0064, 3)
 FAR_COS = fitted(lambda r: np.cos(2 * np.pi * r), 0.25, 6)
 FAR_SIN = fitted(lambda r: np.sin(2 * np.pi * r) / r, 0.25, 6)
 
@@ -74,9 +75,7 @@
 def inner_tables(tile, lags_ref, inner_at):
     lag = jnp.concatenate([lags_ref[tile, c : c + 1, :] for c in range(PT // LANES)], 1)
     cosine, sine = near_turn(jnp.broadcast_to(lag, inner_at.shape) * inner_at)
-    cos_high, cos_low = split(cosine)
-    sin_high, sin_low = split(sine)
-    return lag, (cos_high, sin_high, cos_low, sin_low)
+    return lag, jnp.concatenate(split(jnp.concatenate([cosine, sine], 0)), 0)
 
 
 def outer_tables(tile, lag, drift_ref, turn, frequency, live):
@@ -106,44 +105,50 @@
 
 
 def start_rows(outer):
-    return (lax.broadcasted_iota(jnp.int32, (outer, PT), 0) * INNER).astype(jnp.float32)
+    return (lax.broadcasted_iota(jnp.int32, (outer, PT), 0) * INNER).astype(jnp.float32) + (INNER - 1) / 2
 
 
 def inner_rows():
-    return lax.broadcasted_iota(jnp.int32, (INNER, PT), 0).astype(jnp.float32)
-
-
-def spreading(outer, width):
+    return lax.broadcasted_iota(jnp.int32, (HALF, PT), 0).astype(jnp.float32) + 0.5
+
+
+def spread(rows_ref, band_of, masked, outer, width):
     lane_at = lax.broadcasted_iota(jnp.int32, (outer, width), 1)
     mask = (lane_at // INNER == lax.broadcasted_iota(jnp.int32, (outer, width), 0)).astype(jnp.float32)
-    from_lane = lax.broadcasted_iota(jnp.int32, (width, LANES), 0)
-    to_lane = lax.broadcasted_iota(jnp.int32, (width, LANES), 1)
-    choose = (from_lane % INNER == to_lane % INNER).astype(jnp.float32).astype(jnp.bfloat16)
-    return mask, choose
-
-
-def spread(rows_ref, band_of, masked, outer, width):
-    mask, choose = spreading(outer, width)
+    from_lane = lax.broadcasted_iota(jnp.int32, (width, LANES), 0) % INNER
+    to_lane = lax.broadcasted_iota(jnp.int32, (width, LANES), 1) % HALF
+    choose = jnp.concatenate([from_lane == HALF + to_lane, from_lane == HALF - 1 - to_lane], 1)
 
     def one_slot(slot):
         row = 2 * band_of(slot)
         pair = [jnp.broadcast_to(rows_ref[pl.ds(row + c, 1), :], (outer, width)) * mask for c in range(2)]
-        masked[slot] = jnp.concatenate(pair, 0).astype(jnp.bfloat16)
+        return jnp.concatenate(pair, 0).astype(jnp.bfloat16)
 
     slots = masked.shape[0]
-    over_slots(slots, one_slot)
-    stacked = masked[...].reshape(slots * 2 * outer, width)
-    return jnp.dot(stacked, choose, preferred_element_type=jnp.float32).reshape(slots, 2 * outer, LANES)
+    if slots <= UNROLLED:
+        stacked = jnp.concatenate([one_slot(slot) for slot in range(slots)], 0)
+    else:
+        def kept(slot):
+            masked[slot] = one_slot(slot)
+
+        over_slots(slots, kept)
+        stacked = masked[...].reshape(slots * 2 * outer, width)
+    wide = jnp.dot(stacked, choose.astype(jnp.float32).astype(jnp.bfloat16), preferred_element_type=jnp.float32)
+    wide = wide.reshape(slots, 2 * outer, 2 * LANES)
+    return [wide[:, c * outer : (c + 1) * outer, m * LANES : (m + 1) * LANES] for m in range(2) for c in range(2)]
 
 
 def mix_own(rows_ref, band_of, masked, mixed_ref, s, flip, outer, width):
-    wide = spread(rows_ref, band_of, masked, outer, width)
-    real, imag = wide[:, :outer], wide[:, outer:]
-    even = lax.broadcasted_iota(jnp.int32, real.shape, 2) // INNER % 2 == 0
-    mixed_ref[s, 0] = jnp.where(even, real, -flip * imag)
-    mixed_ref[s, 1] = jnp.where(even, imag, flip * real)
-    mixed_ref[s, 2] = jnp.where(even, -flip * imag, -real)
-    mixed_ref[s, 3] = jnp.where(even, flip * real, -imag)
+    real, imag, real_m, imag_m = spread(rows_ref, band_of, masked, outer, width)
+    even = lax.broadcasted_iota(jnp.int32, real.shape, 2) // HALF % 2 == 0
+    turned, turned_m = flip * imag, flip * imag_m
+    kept, kept_m = flip * real, flip * real_m
+    factors = (
+        (real, -turned), (imag, kept), (real_m, turned_m), (imag_m, -kept_m),
+        (-turned, -real), (kept, -imag), (-turned_m, real_m), (kept_m, imag_m),
+    )
+    for n, (first, second) in enumerate(factors):
+        mixed_ref[s, n] = jnp.where(even, first, second)
 
 
 def power_rows(rows):
@@ -193,7 +198,7 @@
             at = slot * TPB + m
             picks_ref[slots + at : slots + at + 1, :] = jnp.full((1, LANES), tile)
             lag, parts = inner_tables(tile, lags_ref, inner_at)
-            inner_ref[at] = jnp.concatenate(parts, 0)
+            inner_ref[at] = parts
             for s, (live, time) in enumerate(marks):
                 cosine, sine = outer_tables(tile, lag, drift_ref, share * time, frequency, live)
                 outer_ref[at, s, 0] = cosine
@@ -220,7 +225,7 @@
     per_tile = PT // LANES
     slots = masked.shape[0]
     flip = jnp.where(detector_bit == 0, 1.0, -1.0).astype(jnp.float32)
-    part = lax.broadcasted_iota(jnp.int32, (slots, outer, LANES), 2) // INNER
+    part = lax.broadcasted_iota(jnp.int32, (slots, outer, LANES), 2) // HALF
     total[...] = jnp.zeros_like(total)
 
     def band_of(slot):
@@ -246,15 +251,15 @@
             mix_own(rows32, band_of, masked, mixed_ref, s, flip, outer, width)
             inner_at, start_at = inner_rows(), start_rows(outer)
             live, time = clock(valid_ref, tm_count, detector_bit, seg_kept)[s]
-        real, imag = wide[:, :outer], wide[:, outer:]
+        sides = []
         for n in range(2):
-            value = mixed_ref[s, 2 * n] * real + mixed_ref[s, 2 * n + 1] * imag
+            value = sum(mixed_ref[s, 4 * n + q] * wide[q] for q in range(4))
             high = value.astype(jnp.bfloat16).astype(jnp.float32)
-            parts = jnp.where((part == 2) | (part == 3), value - high, high)
-            left[:, n * outer : (n + 1) * outer, :] = parts
+            sides.append(jnp.where((part == 2) | (part == 3), value - high, high))
+        left[...] = jnp.concatenate(sides, 1).astype(jnp.bfloat16)
 
         def one_slot(slot):
-            lhs = left[slot][:, : PARTS * INNER].astype(jnp.bfloat16)
+            lhs = left[slot][:, : PARTS * HALF]
             for m in range(TPB):
                 at = slot * TPB + m
                 tile = tile_of(at)
@@ -263,12 +268,11 @@
                     cosine, sine = outer_ref[at, s, 0], outer_ref[at, s, 1]
                 else:
                     band = band_of(slot) + bin_half * bands_half
-                    lag, parts = inner_tables(tile, lags_ref, inner_at)
-                    table = jnp.concatenate(parts, 0)
+                    lag, table = inner_tables(tile, lags_ref, inner_at)
                     turn = (band.astype(jnp.float32) + 0.5) / (2 * bands_half) * time
                     frequency = (band * width).astype(jnp.float32) + start_at
                     cosine, sine = outer_tables(tile, lag, drift_ref, turn, frequency, live)
-                rhs = jnp.concatenate([table[: 2 * INNER], table], 0)
+                rhs = jnp.concatenate([table[:INNER], table], 0)
                 product = jnp.dot(lhs, rhs, preferred_element_type=jnp.float32)
                 terms = jnp.sum(cosine * product[:outer] - sine * product[outer:], axis=0, keepdims=True)
                 total[s, tile] += jnp.concatenate([terms[:, c * LANES : (c + 1) * LANES] for c in range(per_tile)], 0)
@@ -328,13 +332,13 @@
     held = [pltpu.SMEM(valid.shape, jnp.int32), pltpu.SMEM(table.shape, jnp.int32)]
     held += [pltpu.VMEM(lags.shape, jnp.float32), pltpu.VMEM(drift.shape, jnp.float32)]
     work = [pltpu.VMEM(own.shape[1:], jnp.float32), pltpu.VMEM((slots, 2 * outer, width), jnp.bfloat16)]
-    mixed = jax.ShapeDtypeStruct((seg_kept, 4, slots, outer, LANES), jnp.float32)
+    mixed = jax.ShapeDtypeStruct((seg_kept, 8, slots, outer, LANES), jnp.float32)
     ready = slots <= UNROLLED
     if ready:
         made = pl.pallas_call(
             functools.partial(tables_kernel, tm_count, bands_half, width, seg_kept),
             out_shape=[
-                jax.ShapeDtypeStruct((blocks, 4 * INNER, PT), jnp.bfloat16),
+                jax.ShapeDtypeStruct((blocks, 2 * INNER, PT), jnp.bfloat16),
                 jax.ShapeDtypeStruct((blocks, seg_kept, 2, outer, PT), jnp.float32),
                 mixed,
                 jax.ShapeDtypeStruct((seg_kept, 2, LANES), jnp.float32),
@@ -359,7 +363,7 @@
         scratch_shapes=[
             *held,
             *work,
-            pltpu.VMEM((slots, 2 * outer, LANES), jnp.float32),
+            pltpu.VMEM((slots, 2 * outer, LANES), jnp.bfloat16),
             pltpu.VMEM((seg_kept, pixels // PT, per_tile, LANES), jnp.float32),
         ],
         compiler_params=GRANT if ready else None,

time: 20.7 us -> 20.5 us (level)
  Pallas kernels: 4.06 us -> 3.31 us
  blocking collectives: 13.5 us -> 14 us
    pallas_call x1, Pallas kernels: 2.59 us -> 2.08 us  [shards(): pl.pallas_call(functools.partial(tables_kernel, tm_count, bands_half, wid...]
    all_to_all x1, blocking collectives: 13.5 us -> 14 us  [shards(): received = lax.all_to_all(outgoing, ('det', 'tm'), 0, 0, tiled=True)]
    pallas_call x1, Pallas kernels: 0.83 us -> 0.58 us  [shards(): pl.pallas_call(functools.partial(terms_kernel, tm_count, dests, rows_dest...]
  transfers between devices with their start and end apart: 1 -> 1, of which waited for: 0 -> 0; matrix products, arithmetic and copies ran while one was open for 0% -> 0% of each run, Pallas kernels for 13% -> 10%
where the time goes in v5:
time: 20.5 us; the launch traced here: 20.3 us
  blocking collectives  14 us (68%)
  Pallas kernels  3.31 us (16%)
  starting transfers between devices  3 us (15%)
    all_to_all x1, blocking collectives, shards(): received = lax.all_to_all(outgoing, ('det', 'tm'), 0, 0, tiled=True)  14 us
    ppermute x1, starting transfers between devices, shards(): other = lax.ppermute(own, 'det', [(d, d ^ 2) for d in range(det_count)])  3 us
    pallas_call x1, Pallas kernels, shards(): pl.pallas_call(functools.partial(tables_kernel, tm_count, bands_half, wid...  2.08 us
    pallas_call x1, Pallas kernels, shards(): pl.pallas_call(functools.partial(sum_kernel, tm_count, rows_dest, fourier...  0.65 us
    pallas_call x1, Pallas kernels, shards(): pl.pallas_call(functools.partial(terms_kernel, tm_count, dests, rows_dest...  0.58 us
  transfers between devices with their start and end apart: 1, of which 0 were waited for; matrix products, arithmetic and copies ran while one was open for 0% of the time, Pallas kernels for 10%

profile of v5, /device:TPU:0, one launch (start us, length us, event | category | flops | bytes accessed | tf_op | source)
XLA Modules:
  0.0 20.3 jit_solution(1927527177466487165)
XLA Ops:
  0.0 3.0 %collective-permute-start = (bf16[2,64,128]{2,1,0:T(8,128)(2,1)}, bf16[2,64,128]{2,1,0:T(8,128)(2,1)S(1)}, u32[]{:S(2)}, u32[]{:S(2)}) collective-permute-start(bf16[2,64,128]{2,1,0:T(8,128)(2,1)} %bitcast.7), channel_id=1, source_target_pairs={{0,16},{8,24},{16,0},{24,8},{1,17},{9,25},{17,1},{25,9},{2,18},{10... | collective-permute-start | bytes 98312 | tf_op jit(solution)/shard_map/ppermute | solution.py:328
  3.0 2.1 %tables.1 = (bf16[32,32,512]{2,1,0:T(8,128)(2,1)S(1)}, f32[32,1,2,8,512]{4,3,2,1,0:T(8,128)S(1)}, f32[1,8,16,8,128]{4,3,2,1,0:T(8,128)S(1)}, f32[1,2,128]{2,1,0:T(2,128)S(1)}, s32[48,128]{1,0:T(8,128)S(1)}) custom-call(s32[2]{0:T(128)} %valid_hbm.1, s32[2,64]{1,0:T(2,128)} %bitcast.9, f32[96,4,128]{2,1,0:T(4,128)} %bitcast.5, f32[96,4,128]{2,1,0:T(4,128)} %bitcast.6, ...), custom_call_target="tpu_custom_call" | custom-call | flops 1000000000 | bytes 1000000 | tf_op jit(solution)/shard_map/tables/pallas_call | solution.py:338
  5.1 0.0 collective-permute-done.refs_5_
  5.1 0.6 %terms.1 = bf16[32,1,16,128]{3,2,1,0:T(8,128)(2,1)S(1)} custom-call(bf16[32,32,512]{2,1,0:T(8,128)(2,1)S(1)} %get-tuple-element.10.refs_0_, f32[32,1,2,8,512]{4,3,2,1,0:T(8,128)S(1)} %get-tuple-element.11.refs_1_, f32[1,8,16,8,128]{4,3,2,1,0:T(8,128)S(1)} %get-tuple-element.12.refs_2_, f32[1,2,128]{2,1,0:T(2,128)S(1)} %get-tuple-element.13.refs_3_, ...), custom_call_target="tpu_custom_call" | custom-call | tf_op jit(solution)/shard_map/terms/pallas_call | solution.py:358
  5.7 14.0 %all_to_all.5.got_ref = bf16[32,1,16,128]{3,2,1,0:T(8,128)(2,1)S(1)} all-to-all(bf16[32,1,16,128]{3,2,1,0:T(8,128)(2,1)S(1)} %terms.1), channel_id=1, replica_groups=mesh['det'=4,'tm'=8] {'det','tm'}, dimensions={0} | all-to-all | bytes 262144 | tf_op jit(solution)/shard_map/all_to_all | solution.py:373
  19.7 0.6 %sum.1 = f32[12,128]{1,0:T(8,128)} custom-call(bf16[32,1,16,128]{3,2,1,0:T(8,128)(2,1)S(1)} %all_to_all.5.got_ref), custom_call_target="tpu_custom_call" | custom-call | tf_op jit(solution)/shard_map/sum/pallas_call | solution.py:374
Async XLA Ops:
  0.0 5.1 %collective-permute-start = (bf16[2,64,128]{2,1,0:T(8,128)(2,1)}, bf16[2,64,128]{2,1,0:T(8,128)(2,1)S(1)}, u32[]{:S(2)}, u32[]{:S(2)}) collective-permute-start(bf16[2,64,128]{2,1,0:T(8,128)(2,1)} %bitcast.7), channel_id=1, source_target_pairs={{0,16},{8,24},{16,0},{24,8},{1,17},{9,25},{17,1},{25,9},{2,18},{10... | collective-permute-start | bytes 98312 | tf_op jit(solution)/shard_map/ppermute | solution.py:328

commit v6 on v5

--- a/solution.py
+++ b/solution.py
@@ -8,6 +8,7 @@
 from jax.experimental import pallas as pl
 from jax.experimental.pallas import tpu as pltpu
 from jax.sharding import PartitionSpec as P
+
 
 PT = 512
 TPB = 2
@@ -83,6 +84,11 @@
     shape = frequency.shape
     cosine, sine = any_turn(jnp.broadcast_to(pace * turn, shape) - frequency * jnp.broadcast_to(lag, shape))
     return cosine * live, sine * live
+
+
+def duty():
+    det_index = lax.axis_index("det")
+    return 1 - det_index % 2, det_index // 2
 
 
 def clock(valid_ref, tm_count, detector_bit, seg_kept):
@@ -159,31 +165,14 @@
 
 def tables_kernel(
     tm_count, bands_half, width, seg_kept,
-    valid_hbm, table_hbm, lags_hbm, drift_hbm, own_hbm,
-    inner_ref, outer_ref, mixed_ref, power_ref, picks_ref,
-    valid_ref, table_ref, lags_ref, drift_ref, own_ref, sems, rows32, masked,
+    valid_hbm, table_hbm, lags_hbm, drift_hbm,
+    inner_ref, outer_ref, picks_ref,
+    valid_ref, table_ref, lags_ref, drift_ref, sems,
 ):
-    det_index = lax.axis_index("det")
-    bin_half, detector_bit = det_index % 2, det_index // 2
-    copies = fetch(
-        (table_hbm, own_hbm, valid_hbm, lags_hbm, drift_hbm),
-        (table_ref, own_ref, valid_ref, lags_ref, drift_ref),
-        sems,
-    )
-    outer = width // INNER
-    inner_at, start_at = inner_rows(), start_rows(outer)
-    flip = jnp.where(detector_bit == 0, 1.0, -1.0).astype(jnp.float32)
-    copies[0].wait()
-    copies[1].wait()
-
-    def band_of(slot):
-        return table_ref[0, block_of(slot, table_ref, tm_count, bin_half)] - bin_half * bands_half
-
-    for s in range(seg_kept):
-        rows32[...] = own_ref[detector_bit * seg_kept + s].astype(jnp.float32)
-        power_ref[s] = power_rows(rows32[...])
-        mix_own(rows32, band_of, masked, mixed_ref, s, flip, outer, width)
-    for copy in copies[2:]:
+    bin_half, detector_bit = duty()
+    copies = fetch((valid_hbm, table_hbm, lags_hbm, drift_hbm), (valid_ref, table_ref, lags_ref, drift_ref), sems)
+    inner_at, start_at = inner_rows(), start_rows(width // INNER)
+    for copy in copies:
         copy.wait()
     marks = clock(valid_ref, tm_count, detector_bit, seg_kept)
 
@@ -192,7 +181,7 @@
         band = table_ref[0, row]
         frequency = (band * width).astype(jnp.float32) + start_at
         share = (band.astype(jnp.float32) + 0.5) / (2 * bands_half)
-        picks_ref[slot : slot + 1, :] = jnp.full((1, LANES), band_of(slot))
+        picks_ref[slot : slot + 1, :] = jnp.full((1, LANES), band - bin_half * bands_half)
         for m in range(TPB):
             tile = table_ref[1, row + m]
             at = slot * TPB + m
@@ -208,17 +197,30 @@
     over_slots(slots, one_slot)
 
 
+def mix_kernel(seg_kept, picks_ref, own_ref, mixed_ref, power_ref, rows32, masked):
+    _, detector_bit = duty()
+    _, outer = mixed_ref.shape[2:4]
+    flip = jnp.where(detector_bit == 0, 1.0, -1.0).astype(jnp.float32)
+
+    def band_of(slot):
+        return picks_ref[slot : slot + 1, :][0, 0]
+
+    for s in range(seg_kept):
+        rows32[...] = own_ref[detector_bit * seg_kept + s].astype(jnp.float32)
+        power_ref[s] = power_rows(rows32[...])
+        mix_own(rows32, band_of, masked, mixed_ref, s, flip, outer, own_ref.shape[2])
+
+
 def terms_kernel(tm_count, dests, rows_dest, seg_kept, ready, *refs):
     if ready:
-        inner_ref, outer_ref, mixed_ref, power_ref, picks_ref, other_ref, out_ref, *scratch = refs
+        inner_ref, outer_ref, picks_ref, mixed_ref, power_ref, other_ref, out_ref, *scratch = refs
         copies = ()
     else:
         valid_hbm, table_hbm, lags_hbm, drift_hbm, own_ref, other_ref, out_ref, *scratch = refs
         valid_ref, table_ref, lags_ref, drift_ref, sems, mixed_ref, *scratch = scratch
         copies = fetch((valid_hbm, table_hbm, lags_hbm, drift_hbm), (valid_ref, table_ref, lags_ref, drift_ref), sems)
     rows32, masked, left, total = scratch
-    det_index = lax.axis_index("det")
-    bin_half, detector_bit = det_index % 2, det_index // 2
+    bin_half, detector_bit = duty()
     bands_half = other_ref.shape[1] // 2
     width = other_ref.shape[2]
     outer = width // INNER
@@ -325,7 +327,8 @@
     outer = width // INNER
 
     own = own.reshape(seg_count, 2 * bands_half, width)
-    other = lax.ppermute(own, "det", [(d, d ^ 2) for d in range(det_count)])
+    other = lax.ppermute(own, "det", [(d, d ^ 3) for d in range(det_count)])
+    own = lax.ppermute(own, "det", [(d, d ^ 1) for d in range(det_count)])
     table = block_table.T
     lags, drift = (x.reshape(-1, per_tile, LANES) for x in (lags, drift))
     settings = tuple(pltpu.with_memory_space_constraint(x, pltpu.HBM) for x in (valid, table, lags, drift))
@@ -340,18 +343,26 @@
             out_shape=[
                 jax.ShapeDtypeStruct((blocks, 2 * INNER, PT), jnp.bfloat16),
                 jax.ShapeDtypeStruct((blocks, seg_kept, 2, outer, PT), jnp.float32),
-                mixed,
-                jax.ShapeDtypeStruct((seg_kept, 2, LANES), jnp.float32),
                 jax.ShapeDtypeStruct((slots + blocks, LANES), jnp.int32),
             ],
-            in_specs=[HBM] * 5,
-            out_specs=[VMEM] * 5,
-            scratch_shapes=[*held, pltpu.VMEM(own.shape, own.dtype), pltpu.SemaphoreType.DMA((5,)), *work],
+            in_specs=[HBM] * 4,
+            out_specs=[VMEM] * 3,
+            scratch_shapes=[*held, pltpu.SemaphoreType.DMA((4,))],
             compiler_params=GRANT,
             cost_estimate=pl.CostEstimate(flops=10**9, bytes_accessed=10**6, transcendentals=0),
             name="tables",
-        )(*settings, pltpu.with_memory_space_constraint(own, pltpu.HBM))
-        settings, held = made, []
+        )(*settings)
+        factors = pl.pallas_call(
+            functools.partial(mix_kernel, seg_kept),
+            out_shape=[mixed, jax.ShapeDtypeStruct((seg_kept, 2, LANES), jnp.float32)],
+            in_specs=[VMEM] * 2,
+            out_specs=[VMEM] * 2,
+            scratch_shapes=work,
+            compiler_params=GRANT,
+            cost_estimate=pl.CostEstimate(flops=10**8, bytes_accessed=10**6, transcendentals=0),
+            name="mix",
+        )(made[2], own)
+        settings, held = (*made, *factors), []
     else:
         settings = (*settings, own)
         held += [pltpu.SemaphoreType.DMA((4,)), pltpu.VMEM(mixed.shape, mixed.dtype)]

time: 20.5 us -> 20.2 us (0.985)
  blocking collectives: 14 us -> 13.4 us
    all_to_all x1, blocking collectives: 14 us -> 13.4 us  [shards(): received = lax.all_to_all(outgoing, ('det', 'tm'), 0, 0, tiled=True)]
    ppermute x1 -> x2, starting transfers between devices: 3 us -> 3.11 us  [the longest x1 2.43 us: shards(): other = lax.ppermute(own, 'det', [(d, d ^ 3) for d in range(det_count)])]
  transfers between devices with their start and end apart: 1 -> 2, of which waited for: 0 -> 0; matrix products, arithmetic and copies ran while one was open for 0% -> 0% of each run, Pallas kernels for 10% -> 11%
where the time goes in v6:
time: 20.2 us; the launch traced here: 20.1 us
  blocking collectives  13.4 us (66%)
  Pallas kernels  3.5 us (17%)
  starting transfers between devices  3.11 us (15%)
    all_to_all x1, blocking collectives, shards(): received = lax.all_to_all(outgoing, ('det', 'tm'), 0, 0, tiled=True)  13.4 us
    ppermute x1, starting transfers between devices, shards(): other = lax.ppermute(own, 'det', [(d, d ^ 3) for d in range(det_count)])  2.43 us
    pallas_call x1, Pallas kernels, shards(): pl.pallas_call(functools.partial(tables_kernel, tm_count, bands_half, wid...  2.05 us
    ppermute x1, starting transfers between devices, shards(): own = lax.ppermute(own, 'det', [(d, d ^ 1) for d in range(det_count)])  0.68 us
    pallas_call x1, Pallas kernels, shards(): pl.pallas_call(functools.partial(sum_kernel, tm_count, rows_dest, fourier...  0.65 us
    pallas_call x1, Pallas kernels, shards(): pl.pallas_call(functools.partial(terms_kernel, tm_count, dests, rows_dest...  0.61 us
  transfers between devices with their start and end apart: 2, of which 0 were waited for; matrix products, arithmetic and copies ran while one was open for 0% of the time, Pallas kernels for 11%

profile of v6, /device:TPU:0, one launch (start us, length us, event | category | flops | bytes accessed | tf_op | source)
XLA Modules:
  0.0 20.1 jit_solution(11476601797755400875)
XLA Ops:
  0.0 2.4 %collective-permute-start.1 = (bf16[2,64,128]{2,1,0:T(8,128)(2,1)}, bf16[2,64,128]{2,1,0:T(8,128)(2,1)S(1)}, u32[]{:S(2)}, u32[]{:S(2)}) collective-permute-start(bf16[2,64,128]{2,1,0:T(8,128)(2,1)} %bitcast.7), channel_id=1, source_target_pairs={{0,24},{8,16},{16,8},{24,0},{1,25},{9,17},{17,9},{25,1},{2,26},{10... | collective-permute-start | bytes 98312 | tf_op jit(solution)/shard_map/ppermute | solution.py:330
  2.4 0.7 %collective-permute-start = (bf16[2,64,128]{2,1,0:T(8,128)(2,1)}, bf16[2,64,128]{2,1,0:T(8,128)(2,1)S(1)}, u32[]{:S(2)}, u32[]{:S(2)}) collective-permute-start(bf16[2,64,128]{2,1,0:T(8,128)(2,1)} %bitcast.8), channel_id=1, source_target_pairs={{0,8},{8,0},{16,24},{24,16},{1,9},{9,1},{17,25},{25,17},{2,10},{10... | collective-permute-start | bytes 98312 | tf_op jit(solution)/shard_map/ppermute | solution.py:331
  3.1 2.1 %tables.1 = (bf16[32,32,512]{2,1,0:T(8,128)(2,1)S(1)}, f32[32,1,2,8,512]{4,3,2,1,0:T(8,128)S(1)}, s32[48,128]{1,0:T(8,128)S(1)}) custom-call(s32[2]{0:T(128)} %valid_hbm.1, s32[2,64]{1,0:T(2,128)} %bitcast.9, f32[96,4,128]{2,1,0:T(4,128)} %bitcast.5, f32[96,4,128]{2,1,0:T(4,128)} %bitcast.6), custom_call_target="tpu_custom_call" | custom-call | flops 1000000000 | bytes 1000000 | tf_op jit(solution)/shard_map/tables/pallas_call | solution.py:341
  5.2 0.0 collective-permute-done.own_ref
  5.2 0.2 %mix.1 = (f32[1,8,16,8,128]{4,3,2,1,0:T(8,128)S(1)}, f32[1,2,128]{2,1,0:T(2,128)S(1)}) custom-call(s32[48,128]{1,0:T(8,128)S(1)} %get-tuple-element.12.picks_ref.refs_2_, bf16[2,64,128]{2,1,0:T(8,128)(2,1)S(1)} %collective-permute-done.own_ref), custom_call_target="tpu_custom_call" | custom-call | flops 100000000 | bytes 1000000 | tf_op jit(solution)/shard_map/mix/pallas_call | solution.py:355
  5.4 0.0 collective-permute-done.1.refs_5_
  5.4 0.6 %terms.1 = bf16[32,1,16,128]{3,2,1,0:T(8,128)(2,1)S(1)} custom-call(bf16[32,32,512]{2,1,0:T(8,128)(2,1)S(1)} %get-tuple-element.10.refs_0_, f32[32,1,2,8,512]{4,3,2,1,0:T(8,128)S(1)} %get-tuple-element.11.refs_1_, s32[48,128]{1,0:T(8,128)S(1)} %get-tuple-element.12.picks_ref.refs_2_, f32[1,8,16,8,128]{4,3,2,1,0:T(8,128)S(1)} %get-tuple-element.13.refs_3_, ...), custom_call_target="tpu_custom_call" | custom-call | tf_op jit(solution)/shard_map/terms/pallas_call | solution.py:369
  6.0 13.4 %all_to_all.5.got_ref = bf16[32,1,16,128]{3,2,1,0:T(8,128)(2,1)S(1)} all-to-all(bf16[32,1,16,128]{3,2,1,0:T(8,128)(2,1)S(1)} %terms.1), channel_id=1, replica_groups=mesh['det'=4,'tm'=8] {'det','tm'}, dimensions={0} | all-to-all | bytes 262144 | tf_op jit(solution)/shard_map/all_to_all | solution.py:384
  19.4 0.6 %sum.1 = f32[12,128]{1,0:T(8,128)} custom-call(bf16[32,1,16,128]{3,2,1,0:T(8,128)(2,1)S(1)} %all_to_all.5.got_ref), custom_call_target="tpu_custom_call" | custom-call | tf_op jit(solution)/shard_map/sum/pallas_call | solution.py:385
Async XLA Ops:
  0.0 5.4 %collective-permute-start.1 = (bf16[2,64,128]{2,1,0:T(8,128)(2,1)}, bf16[2,64,128]{2,1,0:T(8,128)(2,1)S(1)}, u32[]{:S(2)}, u32[]{:S(2)}) collective-permute-start(bf16[2,64,128]{2,1,0:T(8,128)(2,1)} %bitcast.7), channel_id=1, source_target_pairs={{0,24},{8,16},{16,8},{24,0},{1,25},{9,17},{17,9},{25,1},{2,26},{10... | collective-permute-start | bytes 98312 | tf_op jit(solution)/shard_map/ppermute | solution.py:330
  2.4 2.7 %collective-permute-start = (bf16[2,64,128]{2,1,0:T(8,128)(2,1)}, bf16[2,64,128]{2,1,0:T(8,128)(2,1)S(1)}, u32[]{:S(2)}, u32[]{:S(2)}) collective-permute-start(bf16[2,64,128]{2,1,0:T(8,128)(2,1)} %bitcast.8), channel_id=1, source_target_pairs={{0,8},{8,0},{16,24},{24,16},{1,9},{9,1},{17,25},{25,17},{2,10},{10... | collective-permute-start | bytes 98312 | tf_op jit(solution)/shard_map/ppermute | solution.py:331

commit v7 on v6

--- a/solution.py
+++ b/solution.py
@@ -118,7 +118,7 @@
     return lax.broadcasted_iota(jnp.int32, (HALF, PT), 0).astype(jnp.float32) + 0.5
 
 
-def spread(rows_ref, band_of, masked, outer, width):
+def spread(rows_ref, band_of, masked, outer, width, gather=False):
     lane_at = lax.broadcasted_iota(jnp.int32, (outer, width), 1)
     mask = (lane_at // INNER == lax.broadcasted_iota(jnp.int32, (outer, width), 0)).astype(jnp.float32)
     from_lane = lax.broadcasted_iota(jnp.int32, (width, LANES), 0) % INNER
@@ -131,6 +131,16 @@
         return jnp.concatenate(pair, 0).astype(jnp.bfloat16)
 
     slots = masked.shape[0]
+    if slots <= UNROLLED and gather:
+        at = lax.broadcasted_iota(jnp.int32, (outer, LANES), 0) * INNER
+        lane = lax.broadcasted_iota(jnp.int32, (outer, LANES), 1) % HALF
+        sources = (at + HALF + lane, at + HALF - 1 - lane)
+        rows = [[jnp.broadcast_to(rows_ref[pl.ds(2 * band_of(slot) + c, 1), :], (outer, width)) for c in range(2)] for slot in range(slots)]
+        return [
+            jnp.stack([jnp.take_along_axis(pair[c], source, axis=1, mode="promise_in_bounds") for pair in rows])
+            for source in sources
+            for c in range(2)
+        ]
     if slots <= UNROLLED:
         stacked = jnp.concatenate([one_slot(slot) for slot in range(slots)], 0)
     else:
@@ -247,7 +257,7 @@
         if s == 0:
             for copy in copies:
                 copy.wait()
-        wide = spread(rows32, band_of, masked, outer, width)
+        wide = spread(rows32, band_of, masked, outer, width, gather=ready)
         if not ready:
             rows32[...] = own_ref[seg].astype(jnp.float32)
             mix_own(rows32, band_of, masked, mixed_ref, s, flip, outer, width)

time: 20.2 us -> 20.2 us (level)
  no operation moved by 1% of the time
where the time goes in v7:
time: 20.2 us; the launch traced here: 20 us
  blocking collectives  13.4 us (66%)
  Pallas kernels  3.4 us (17%)
  starting transfers between devices  3.11 us (15%)
    all_to_all x1, blocking collectives, shards(): received = lax.all_to_all(outgoing, ('det', 'tm'), 0, 0, tiled=True)  13.4 us
    ppermute x1, starting transfers between devices, shards(): other = lax.ppermute(own, 'det', [(d, d ^ 3) for d in range(det_count)])  2.43 us
    pallas_call x1, Pallas kernels, shards(): pl.pallas_call(functools.partial(tables_kernel, tm_count, bands_half, wid...  2.05 us
    ppermute x1, starting transfers between devices, shards(): own = lax.ppermute(own, 'det', [(d, d ^ 1) for d in range(det_count)])  0.68 us
    pallas_call x1, Pallas kernels, shards(): pl.pallas_call(functools.partial(sum_kernel, tm_count, rows_dest, fourier...  0.65 us
    pallas_call x1, Pallas kernels, shards(): pl.pallas_call(functools.partial(terms_kernel, tm_count, dests, rows_dest...  0.51 us
  transfers between devices with their start and end apart: 2, of which 0 were waited for; matrix products, arithmetic and copies ran while one was open for 0% of the time, Pallas kernels for 11%

profile of v7, /device:TPU:0, one launch (start us, length us, event | category | flops | bytes accessed | tf_op | source)
XLA Modules:
  0.0 20.0 jit_solution(6122463951772075648)
XLA Ops:
  0.0 2.4 %collective-permute-start.1 = (bf16[2,64,128]{2,1,0:T(8,128)(2,1)}, bf16[2,64,128]{2,1,0:T(8,128)(2,1)S(1)}, u32[]{:S(2)}, u32[]{:S(2)}) collective-permute-start(bf16[2,64,128]{2,1,0:T(8,128)(2,1)} %bitcast.7), channel_id=1, source_target_pairs={{0,24},{8,16},{16,8},{24,0},{1,25},{9,17},{17,9},{25,1},{2,26},{10... | collective-permute-start | bytes 98312 | tf_op jit(solution)/shard_map/ppermute | solution.py:340
  2.4 0.7 %collective-permute-start = (bf16[2,64,128]{2,1,0:T(8,128)(2,1)}, bf16[2,64,128]{2,1,0:T(8,128)(2,1)S(1)}, u32[]{:S(2)}, u32[]{:S(2)}) collective-permute-start(bf16[2,64,128]{2,1,0:T(8,128)(2,1)} %bitcast.8), channel_id=1, source_target_pairs={{0,8},{8,0},{16,24},{24,16},{1,9},{9,1},{17,25},{25,17},{2,10},{10... | collective-permute-start | bytes 98312 | tf_op jit(solution)/shard_map/ppermute | solution.py:341
  3.1 2.1 %tables.1 = (bf16[32,32,512]{2,1,0:T(8,128)(2,1)S(1)}, f32[32,1,2,8,512]{4,3,2,1,0:T(8,128)S(1)}, s32[48,128]{1,0:T(8,128)S(1)}) custom-call(s32[2]{0:T(128)} %valid_hbm.1, s32[2,64]{1,0:T(2,128)} %bitcast.9, f32[96,4,128]{2,1,0:T(4,128)} %bitcast.5, f32[96,4,128]{2,1,0:T(4,128)} %bitcast.6), custom_call_target="tpu_custom_call" | custom-call | flops 1000000000 | bytes 1000000 | tf_op jit(solution)/shard_map/tables/pallas_call | solution.py:351
  5.2 0.0 collective-permute-done.own_ref
  5.2 0.2 %mix.1 = (f32[1,8,16,8,128]{4,3,2,1,0:T(8,128)S(1)}, f32[1,2,128]{2,1,0:T(2,128)S(1)}) custom-call(s32[48,128]{1,0:T(8,128)S(1)} %get-tuple-element.12.picks_ref.refs_2_, bf16[2,64,128]{2,1,0:T(8,128)(2,1)S(1)} %collective-permute-done.own_ref), custom_call_target="tpu_custom_call" | custom-call | flops 100000000 | bytes 1000000 | tf_op jit(solution)/shard_map/mix/pallas_call | solution.py:365
  5.4 0.0 collective-permute-done.1.refs_5_
  5.4 0.5 %terms.1 = bf16[32,1,16,128]{3,2,1,0:T(8,128)(2,1)S(1)} custom-call(bf16[32,32,512]{2,1,0:T(8,128)(2,1)S(1)} %get-tuple-element.10.refs_0_, f32[32,1,2,8,512]{4,3,2,1,0:T(8,128)S(1)} %get-tuple-element.11.refs_1_, s32[48,128]{1,0:T(8,128)S(1)} %get-tuple-element.12.picks_ref.refs_2_, f32[1,8,16,8,128]{4,3,2,1,0:T(8,128)S(1)} %get-tuple-element.13.refs_3_, ...), custom_call_target="tpu_custom_call" | custom-call | tf_op jit(solution)/shard_map/terms/pallas_call | solution.py:379
  5.9 13.4 %all_to_all.5.got_ref = bf16[32,1,16,128]{3,2,1,0:T(8,128)(2,1)S(1)} all-to-all(bf16[32,1,16,128]{3,2,1,0:T(8,128)(2,1)S(1)} %terms.1), channel_id=1, replica_groups=mesh['det'=4,'tm'=8] {'det','tm'}, dimensions={0} | all-to-all | bytes 262144 | tf_op jit(solution)/shard_map/all_to_all | solution.py:394
  19.3 0.6 %sum.1 = f32[12,128]{1,0:T(8,128)} custom-call(bf16[32,1,16,128]{3,2,1,0:T(8,128)(2,1)S(1)} %all_to_all.5.got_ref), custom_call_target="tpu_custom_call" | custom-call | tf_op jit(solution)/shard_map/sum/pallas_call | solution.py:395
Async XLA Ops:
  0.0 5.4 %collective-permute-start.1 = (bf16[2,64,128]{2,1,0:T(8,128)(2,1)}, bf16[2,64,128]{2,1,0:T(8,128)(2,1)S(1)}, u32[]{:S(2)}, u32[]{:S(2)}) collective-permute-start(bf16[2,64,128]{2,1,0:T(8,128)(2,1)} %bitcast.7), channel_id=1, source_target_pairs={{0,24},{8,16},{16,8},{24,0},{1,25},{9,17},{17,9},{25,1},{2,26},{10... | collective-permute-start | bytes 98312 | tf_op jit(solution)/shard_map/ppermute | solution.py:340
  2.4 2.7 %collective-permute-start = (bf16[2,64,128]{2,1,0:T(8,128)(2,1)}, bf16[2,64,128]{2,1,0:T(8,128)(2,1)S(1)}, u32[]{:S(2)}, u32[]{:S(2)}) collective-permute-start(bf16[2,64,128]{2,1,0:T(8,128)(2,1)} %bitcast.8), channel_id=1, source_target_pairs={{0,8},{8,0},{16,24},{24,16},{1,9},{9,1},{17,25},{25,17},{2,10},{10... | collective-permute-start | bytes 98312 | tf_op jit(solution)/shard_map/ppermute | solution.py:341
